TPU v7x, 128 devices: a whole 4x4x4 slice. The times are simulated.
128 devices in a mesh: grp: 4 (over z), dev: 32 (over y, x, core).
Axes of the slice: x: 4, y: 4, z: 4, core: 2. Of those that a mesh axis runs over, the one named last changes fastest.
Arguments:
- omega: float32 [4, 128, 256, 128], P('grp', 'dev'), may hold values from -6 to 6
- u_factor: float32 [4, 128, 80, 256, 32], P('grp', 'dev'), may hold values from -0.0625 to 0.0625
- v_factor: float32 [4, 128, 80, 256, 32], P('grp', 'dev'), may hold values from -0.375 to 0.375
- columns: int32 [4, 128, 80, 1], P('grp', 'dev'), may hold values from 0 to 127; in each aligned block of 320 rows (0 to 319, 320 to 639, ..., all dimensions but the last counted through in order) at most 3 rows name the same one
- ranks: int32 [4, 128, 80], P('grp', 'dev'), may hold values from 8 to 32
Outputs:
- leaf_basis: float32 [128, 256, 128], P('dev', 'grp')
- transfer: float32 [128, 256, 128], P('dev')
Inputs may be any that keep to these rules, and one draw needn't show every extreme that they name: `columns`: within the 320 blocks of one device's row clusters in one group, at most 3 name any one column cluster, and some column cluster is named by exactly 3.
All inputs are finite; a program needn't handle non-finite values.
Results may differ from a plain program's by a relative error of at most 0.0003.
Values sent between devices are 32-bit elements; how exact they have to be, the bound alone decides.
A program may use at most 192 MiB of HBM per device.

v0:
```python
import jax
import jax.numpy as jnp
from jax import lax
from jax.sharding import PartitionSpec as P

precise = lax.Precision.HIGHEST


def split_up(value, dim, count):
    dims = value.shape
    pieces = value.reshape(*dims[:dim], count, dims[dim] // count, *dims[dim + 1 :])
    return jnp.moveaxis(pieces, dim, 0)


def sum_at_owner(value, axis, dim):
    pieces = split_up(value, dim, lax.axis_size(axis))
    arrived = lax.all_to_all(pieces, axis, split_axis=0, concat_axis=0, tiled=True)
    return arrived.sum(axis=0)


def copy_for_each(value, axis):
    copies = jnp.broadcast_to(value, (lax.axis_size(axis), *value.shape))
    return lax.all_to_all(copies, axis, split_axis=0, concat_axis=0, tiled=True)


def taken_together(value, axis):
    return copy_for_each(value, axis).sum(axis=0)


def swapped(value, axis, apart):
    mask = 2**apart
    pairs = [(source, source ^ mask) for source in range(lax.axis_size(axis))]
    return lax.ppermute(value, axis, pairs)


def on_device(omega, u_factor, v_factor, columns, ranks):
    n_local = u_factor.shape[1]
    n_blocks = u_factor.shape[2]
    leaf_rows = u_factor.shape[3]
    rank_width = u_factor.shape[4]
    probe_count = omega.shape[3]
    dev_count = lax.axis_size("dev")
    col_flat = columns[0, :, :, 0].reshape(n_local * n_blocks)
    v_flat = v_factor[0].reshape(n_local * n_blocks, leaf_rows, rank_width)
    whole_probe = lax.all_gather(omega, "dev", axis=1, tiled=True)[0]
    coeff = jnp.einsum("bik,bip->bkp", v_flat, whole_probe[col_flat], precision=precise)
    rank_mask = (
        jnp.arange(rank_width, dtype=jnp.int32)[None, None, :] < ranks[0][:, :, None]
    ).astype(jnp.float32)
    masked_rows = u_factor[0] * rank_mask[:, :, None, :]
    partial_sketch = jnp.einsum(
        "cbik,cbkp->cip",
        masked_rows,
        coeff.reshape(n_local, n_blocks, rank_width, probe_count),
        precision=precise,
    )
    own_rows = sum_at_owner(partial_sketch, "grp", 1)
    gram_matrix = taken_together(
        jnp.einsum("cip,ciq->cpq", own_rows, own_rows, precision=precise), "grp"
    )
    pair_gram = gram_matrix[0::2] + gram_matrix[1::2]
    top_gram = pair_gram[0] + pair_gram[1]
    device_index = lax.axis_index("dev")
    tree_bits = dev_count.bit_length() - 1
    identity = jnp.eye(probe_count, dtype=jnp.float32)
    keep_left = identity
    keep_right = identity
    owned = device_index < 0
    current = top_gram
    for depth_step in range(tree_bits):
        sibling = swapped(current, "dev", depth_step)
        is_left = device_index // 2**depth_step % 2 == 0
        left_gram = jnp.where(is_left, current, sibling)
        right_gram = jnp.where(is_left, sibling, current)
        owner = device_index % 2 ** (depth_step + 1) == 2**depth_step - 1
        keep_left = jnp.where(owner, left_gram, keep_left)
        keep_right = jnp.where(owner, right_gram, keep_right)
        owned = jnp.logical_or(owned, owner)
        current = left_gram + right_gram
    all_grams = jnp.concatenate(
        [
            gram_matrix,
            pair_gram,
            top_gram[None],
            keep_left[None],
            keep_right[None],
            (keep_left + keep_right)[None],
        ],
        axis=0,
    )
    all_lower = jnp.linalg.cholesky(all_grams)
    all_upper = jnp.swapaxes(all_lower, 1, 2)
    leaf_basis = lax.linalg.triangular_solve(
        all_lower[0:4], own_rows, left_side=False, lower=True, transpose_a=True
    )
    left_parts = jnp.stack([all_upper[0], all_upper[2], all_upper[4], all_upper[7]], axis=0)
    right_parts = jnp.stack([all_upper[1], all_upper[3], all_upper[5], all_upper[8]], axis=0)
    parent_lower = jnp.stack([all_lower[4], all_lower[5], all_lower[6], all_lower[9]], axis=0)
    stacked_rows = jnp.concatenate([left_parts, right_parts], axis=1)
    node_transfer = lax.linalg.triangular_solve(
        parent_lower, stacked_rows, left_side=False, lower=True, transpose_a=True
    )
    kept = jnp.where(owned, node_transfer[3], jnp.zeros_like(node_transfer[3]))
    transfer = jnp.stack([node_transfer[0], node_transfer[1], node_transfer[2], kept], axis=0)
    return (leaf_basis, transfer)


def solution(mesh):
    placed = (
        P("grp", "dev", None, None),
        P("grp", "dev", None, None, None),
        P("grp", "dev", None, None, None),
        P("grp", "dev", None, None),
        P("grp", "dev", None),
    )
    return jax.shard_map(
        on_device,
        mesh=mesh,
        in_specs=placed,
        out_specs=(P("dev", "grp", None), P("dev", None, None)),
        check_vma=False,
    )
```

profile of v0, /device:TPU:0, one launch (start us, length us, event | category | flops | bytes accessed | tf_op | source)
XLA Modules:
  0.0 419.6 jit_solution(14103406763547813062)
XLA Ops:
  7.2 0.0 all-gather.2.cloned.1.call-start
  7.2 0.7 all-gather.2.cloned.1.call-update
  7.9 0.5 broadcast.119
  8.4 1.3 reduce.11
  9.8 0.1 reshape_squeeze.6
  9.9 0.8 fusion.23
  10.7 74.5 %all-gather.2.cloned.1.call-done = f32[1,128,256,128]{3,2,0,1:T(8,128)} async-done(((f32[1,4,256,128]{3,2,0,1:T(8,128)}), f32[1,128,256,128]{3,2,0,1:T(8,128)}) %all-gather.2.cloned.1.call-update) | async-done | bytes 16777232 | tf_op jit(solution)/shard_map/all_gather | solution.py:45
  85.2 23.4 %gather_fusion = f32[320,256,128]{2,1,0:T(8,128)} fusion(f32[128,256,128]{2,1,0:T(8,128)} %bitcast.54, s32[1024]{0:T(1024)S(1)} %pad_clamp_fusion), kind=kCustom, calls=%fused_computation | custom fusion | bytes 83887360 | tf_op jit(solution)/shard_map/gather | solution.py:46
  108.5 0.0 copy-start
  108.5 31.4 %fusion.43 = f32[320,128,32]{1,2,0:T(8,128)S(1)} fusion(f32[320,256,128]{2,1,0:T(8,128)} %gather_fusion, f32[320,256,32]{1,2,0:T(8,128)} %bitcast.55), kind=kOutput, calls=%fused_computation.76 | convolution fusion | flops 4026531840 | bytes 57671680 | tf_op jit(solution)/shard_map/bik,bip->bkp/dot_general | solution.py:46
  139.9 0.0 copy-done
  139.9 18.2 %fusion = f32[4,256,128,1]{2,1,3,0:T(8,128)S(1)} fusion(f32[4,80,32,128]{3,2,1,0:T(8,128)S(1)} %bitcast.56, f32[1,4,80,256,32]{3,4,2,1,0:T(8,128)S(1)} %copy-done, f32[4,80,32]{2,1,0:T(8,128)S(1)} %fusion.23), kind=kOutput, calls=%fused_computation.2 | convolution fusion | flops 4029153280 | bytes 16293888 | tf_op jit(solution)/shard_map/cbik,cbkp->cip/dot_general | solution.py:51
  158.2 14.1 %all_to_all.10 = f32[4,4,64,128]{3,2,1,0:T(8,128)S(1)} all-to-all(f32[4,4,64,128]{3,2,1,0:T(8,128)S(1)} %bitcast.57), channel_id=1, replica_groups=mesh['grp'=4,'dev'=32] {'grp'}, dimensions={0} | all-to-all | bytes 1048576 | tf_op jit(solution)/shard_map/all_to_all | solution.py:17
  172.4 0.6 fusion.44
  172.9 0.1 broadcast_in_dim.26
  173.1 17.1 %all_to_all.11 = f32[4,4,128,128]{3,2,1,0:T(8,128)S(1)} all-to-all(f32[4,4,128,128]{3,2,1,0:T(8,128)S(1)} %broadcast_in_dim.26), channel_id=1, replica_groups=mesh['grp'=4,'dev'=32] {'grp'}, dimensions={0} | all-to-all | bytes 2097152 | tf_op jit(solution)/shard_map/all_to_all | solution.py:23
  190.1 0.1 reduce_sum.19
  190.2 0.1 copy.32
  190.4 0.1 collective-permute-start
  190.5 1.2 collective-permute-done
  191.8 1.5 collective-permute-start.1
  193.3 2.8 collective-permute-done.1
  196.1 3.0 collective-permute-start.2
  199.2 2.8 collective-permute-done.2
  202.0 1.2 collective-permute-start.3
  203.2 0.1 copy.29
  203.3 3.0 collective-permute-done.3
  206.4 2.7 collective-permute-start.4
  209.1 3.2 collective-permute-done.4
  212.3 0.1 bitcast_dynamic-update-slice_fusion.1
  212.3 0.2 copy.33
  212.6 0.1 fusion.2
  212.7 117.5 %custom-call.10 = f32[10,128,128]{2,1,0:T(8,128)S(1)} custom-call(f32[10,128,128]{2,1,0:T(8,128)S(1)} %fusion.2), custom_call_target="Cholesky" | custom-call | tf_op jit(solution)/shard_map/jit(cholesky)/cholesky | solution.py:91
  330.1 0.1 select_reduce_fusion
  330.2 0.1 compare_reduce_fusion
  330.3 0.1 select_select_fusion
  330.5 0.1 fusion.51
  330.7 39.3 %custom-call.11 = f32[4,1,128,128]{2,3,1,0:T(8,128)S(1)} custom-call(f32[4,1,128,128]{3,2,1,0:T(8,128)S(1)} %fusion.19), custom_call_target="InvertDiagBlocksLowerTriangular" | custom-call | tf_op jit(solution)/shard_map/triangular_solve | solution.py:93
  370.0 1.0 fusion.21
  371.1 39.3 %custom-call.12 = f32[4,1,128,128]{2,3,1,0:T(8,128)S(1)} custom-call(f32[4,1,128,128]{3,2,1,0:T(8,128)S(1)} %maximum_select_fusion), custom_call_target="InvertDiagBlocksLowerTriangular" | custom-call | tf_op jit(solution)/shard_map/triangular_solve | solution.py:100
  410.4 1.0 fusion.3
  411.5 0.8 pad_maximum_fusion
  (22 shorter events, 0.4 us)
Async XLA Ops:
  7.2 78.0 %all-gather.2.cloned.1.call-start = ((), (), s32[]{:S(2)}) async-start(), calls=%async_computation.2 | async-start | bytes 17301504 | tf_op jit(solution)/shard_map/all_gather | solution.py:45
  108.5 31.4 %copy-start = (f32[1,4,80,256,32]{3,4,2,1,0:T(8,128)S(1)}, f32[1,4,80,256,32]{3,4,2,1,0:T(8,128)}, u32[]{:S(2)}) copy-start(f32[1,4,80,256,32]{3,4,2,1,0:T(8,128)} %param.6) | copy-start | bytes 31457284
  190.4 1.3 collective-permute-start
  191.8 4.3 %collective-permute-start.1 = (f32[128,128]{0,1:T(8,128)S(1)}, f32[128,128]{0,1:T(8,128)S(1)}, u32[]{:S(2)}, u32[]{:S(2)}) collective-permute-start(f32[128,128]{0,1:T(8,128)S(1)} %fusion.32), channel_id=1, source_target_pairs={{0,2},{1,3},{2,0},{3,1},{4,6},{5,7},{6,4},{7,5},{8,10},{9,11},{10,... | collective-permute-start | bytes 196616 | tf_op jit(solution)/shard_map/ppermute | solution.py:33
  196.1 5.8 %collective-permute-start.2 = (f32[128,128]{0,1:T(8,128)S(1)}, f32[128,128]{0,1:T(8,128)S(1)}, u32[]{:S(2)}, u32[]{:S(2)}) collective-permute-start(f32[128,128]{0,1:T(8,128)S(1)} %fusion.35), channel_id=1, source_target_pairs={{0,4},{1,5},{2,6},{3,7},{4,0},{5,1},{6,2},{7,3},{8,12},{9,13},{10,... | collective-permute-start | bytes 196616 | tf_op jit(solution)/shard_map/ppermute | solution.py:33
  202.0 4.3 %collective-permute-start.3 = (f32[128,128]{0,1:T(8,128)S(1)}, f32[128,128]{0,1:T(8,128)S(1)}, u32[]{:S(2)}, u32[]{:S(2)}) collective-permute-start(f32[128,128]{0,1:T(8,128)S(1)} %fusion.34), channel_id=1, source_target_pairs={{0,8},{1,9},{2,10},{3,11},{4,12},{5,13},{6,14},{7,15},{8,0},{9,1},... | collective-permute-start | bytes 196616 | tf_op jit(solution)/shard_map/ppermute | solution.py:33
  206.4 5.8 %collective-permute-start.4 = (f32[128,128]{0,1:T(8,128)S(1)}, f32[128,128]{0,1:T(8,128)S(1)}, u32[]{:S(2)}, u32[]{:S(2)}) collective-permute-start(f32[128,128]{0,1:T(8,128)S(1)} %fusion.33), channel_id=1, source_target_pairs={{0,16},{1,17},{2,18},{3,19},{4,20},{5,21},{6,22},{7,23},{8,24},{9,... | collective-permute-start | bytes 196616 | tf_op jit(solution)/shard_map/ppermute | solution.py:33
Sparse Core Ops, SparseCore 0:
  10.2 74.8 all-gather.1
where the time goes:
time: 426 us; the launch traced here: 420 us
  other arithmetic  200 us (47%)
  waiting for transfers between devices  88.2 us (21%)
  matrix products  52.2 us (12%)
  blocking collectives  31.2 us (7%)
  local copies, waits for them, and re-layouts  24.7 us (6%)
  between operations  14.8 us (3%)
  starting transfers between devices  8.53 us (2%)
    another operation x4, other arithmetic, on_device(): all_lower = jnp.linalg.cholesky(all_grams)  118 us
    all_gather x1, waiting for transfers between devices, on_device(): whole_probe = lax.all_gather(omega, 'dev', axis=1, tiled=True)[0]  74.5 us
    another operation x3, other arithmetic, on_device(): lax.linalg.triangular_solve(all_lower[0:4], own_rows, left_side=False, lo...  39.4 us
    another operation x2, other arithmetic, on_device(): lax.linalg.triangular_solve(parent_lower, stacked_rows, left_side=False,...  39.3 us
    dot_general x1, matrix products, on_device(): jnp.einsum('bik,bip->bkp', v_flat, whole_probe[col_flat], precision=precise)  31.4 us
    gather x1, local copies, waits for them, and re-layouts, on_device(): whole_probe[col_flat]  23.4 us
    dot_general x1, matrix products, on_device(): jnp.einsum('cbik,cbkp->cip', masked_rows, coeff.reshape(n_local, n_blocks...  18.2 us
    all_to_all x1, blocking collectives, copy_for_each(): return lax.all_to_all(copies, axis, split_axis=0, concat_axis=0, tiled=True)  17.1 us
  transfers between devices with their start and end apart: 6, of which 6 were waited for; matrix products, arithmetic and copies ran while one was open for 1% of the time, Pallas kernels for 0%

commit v1 on v0

--- a/solution.py
+++ b/solution.py
@@ -1,9 +1,124 @@
+import functools
 import jax
 import jax.numpy as jnp
 from jax import lax
+from jax.experimental import pallas as pl
+from jax.experimental.pallas import tpu as pltpu
 from jax.sharding import PartitionSpec as P
 
 precise = lax.Precision.HIGHEST
+fast = lax.Precision.HIGH
+
+
+GROUP = 5
+SEGS = ((0, 4), (4, 8), (8, 12), (12, 16))
+
+def pick_lane(x, lane):
+    idx = jnp.full(x.shape, lane, jnp.int32)
+    return jnp.take_along_axis(x, idx, axis=1)
+
+def factor_all(work, mats):
+    sub = lax.broadcasted_iota(jnp.int32, (8, 128), 0)
+    lane = lax.broadcasted_iota(jnp.int32, (8, 128), 1)
+
+    def split(x):
+        h = x.astype(jnp.bfloat16).astype(jnp.float32)
+        rest = x - h
+        d = rest.astype(jnp.bfloat16).astype(jnp.float32)
+        return h, d, rest - d
+
+    def panel(k, top):
+        base = pl.multiple_of(k * 8, 8)
+        raw = [work[m, pl.ds(base, 8), :] for m in mats]
+        keep = lane >= base + sub
+        below = lane >= base + 8
+        prods = []
+        rows = []
+        for g in range(0, len(mats), GROUP):
+            part = raw[g:g + GROUP]
+            ps = [x[:, 0:128] for x in part]
+            qs = [x[:, 128:256] for x in part]
+            cols = [[pick_lane(p, base + r) for r in range(8)] for p in ps]
+            for r in range(8):
+                for i in range(len(part)):
+                    c = cols[i][r]
+                    inv = lax.rsqrt(jnp.broadcast_to(c[r:r + 1], (8, 128)))
+                    cs = c * inv
+                    prow = ps[i][r:r + 1] * inv
+                    qrow = qs[i][r:r + 1] * inv
+                    cz = jnp.where(sub > r, cs, 0.0)
+                    ps[i] = jnp.where(sub == r, prow, ps[i] - cz * prow)
+                    qs[i] = jnp.where(sub == r, qrow, qs[i] - cz * qrow)
+                    for t in range(r + 1, 8):
+                        cols[i][t] = cols[i][t] - cs * cs[t:t + 1]
+            for i in range(len(part)):
+                p = jnp.where(keep, ps[i], 0.0)
+                full = jnp.concatenate([p, qs[i]], axis=1)
+                rows.append(full)
+                ph, pd, pe = split(jnp.where(below, p, 0.0))
+                fh, fd, fe = split(full)
+                left = jnp.concatenate([ph, ph, pd, ph, pe, pd], axis=0)
+                right = jnp.concatenate([fh, fd, fh, fe, fh, fd], axis=0)
+                leftT = left.T[top:].astype(jnp.bfloat16)
+                prods.append(lax.dot_general(leftT, right.astype(jnp.bfloat16), (((1,), (0,)), ((), ())), preferred_element_type=jnp.float32))
+        for m, full, prod in zip(mats, rows, prods):
+            work[m, pl.ds(base, 8), :] = full
+        for m, full, prod in zip(mats, rows, prods):
+            work[m, top:128, :] = work[m, top:128, :] - prod
+
+    for lo, hi in SEGS:
+        def body(k, _, lo=lo):
+            panel(k, lo * 8)
+            return 0
+        lax.fori_loop(lo, hi, body, 0)
+
+def init_work(work, m, gram):
+    r = lax.broadcasted_iota(jnp.int32, (128, 128), 0)
+    c = lax.broadcasted_iota(jnp.int32, (128, 128), 1)
+    work[m, :, 0:128] = gram
+    work[m, :, 128:256] = jnp.where(r == c, 1.0, 0.0)
+
+
+NODES = ((0, 1, 4), (2, 3, 5), (4, 5, 6), (7, 8, 9))
+
+
+def times_transposed(x, y):
+    return lax.dot_general(x, y, (((1,), (1,)), ((), ())), precision=precise, preferred_element_type=jnp.float32)
+
+
+def write_outputs(work, rows, basis_ref, transfer_ref):
+    for c in range(4):
+        basis_ref[c] = times_transposed(rows[c], work[c, :, 128:256])
+    last = lax.axis_index("dev") == lax.axis_size("dev") - 1
+    for n, (left, right, parent) in enumerate(NODES):
+        inverse = work[parent, :, 128:256]
+        for half, child in enumerate((left, right)):
+            made = times_transposed(work[child, :, 0:128], inverse)
+            if n == 3:
+                made = jnp.where(last, 0.0, made)
+            transfer_ref[n, half * 128 : (half + 1) * 128, :] = made
+
+
+def factor_kernel(gram_ref, rows_ref, basis_ref, transfer_ref, work):
+    for m in range(10):
+        init_work(work, m, gram_ref[m])
+    factor_all(work, range(10))
+    write_outputs(work, [rows_ref[c] for c in range(4)], basis_ref, transfer_ref)
+
+
+def factor(grams, rows):
+    vmem = pl.BlockSpec(memory_space=pltpu.VMEM)
+    return pl.pallas_call(
+        factor_kernel,
+        out_shape=(
+            jax.ShapeDtypeStruct((4, 64, 128), jnp.float32),
+            jax.ShapeDtypeStruct((4, 256, 128), jnp.float32),
+        ),
+        in_specs=[vmem, vmem],
+        out_specs=(vmem, vmem),
+        scratch_shapes=[pltpu.VMEM((10, 128, 256), jnp.float32)],
+        name="factor",
+    )(grams, rows)
 
 
 def split_up(value, dim, count):
@@ -43,7 +158,7 @@
     col_flat = columns[0, :, :, 0].reshape(n_local * n_blocks)
     v_flat = v_factor[0].reshape(n_local * n_blocks, leaf_rows, rank_width)
     whole_probe = lax.all_gather(omega, "dev", axis=1, tiled=True)[0]
-    coeff = jnp.einsum("bik,bip->bkp", v_flat, whole_probe[col_flat], precision=precise)
+    coeff = jnp.einsum("bik,bip->bkp", v_flat, whole_probe[col_flat], precision=fast)
     rank_mask = (
         jnp.arange(rank_width, dtype=jnp.int32)[None, None, :] < ranks[0][:, :, None]
     ).astype(jnp.float32)
@@ -52,7 +167,7 @@
         "cbik,cbkp->cip",
         masked_rows,
         coeff.reshape(n_local, n_blocks, rank_width, probe_count),
-        precision=precise,
+        precision=fast,
     )
     own_rows = sum_at_owner(partial_sketch, "grp", 1)
     gram_matrix = taken_together(
@@ -62,10 +177,8 @@
     top_gram = pair_gram[0] + pair_gram[1]
     device_index = lax.axis_index("dev")
     tree_bits = dev_count.bit_length() - 1
-    identity = jnp.eye(probe_count, dtype=jnp.float32)
-    keep_left = identity
-    keep_right = identity
-    owned = device_index < 0
+    keep_left = jnp.eye(probe_count, dtype=jnp.float32)
+    keep_right = keep_left
     current = top_gram
     for depth_step in range(tree_bits):
         sibling = swapped(current, "dev", depth_step)
@@ -75,7 +188,6 @@
         owner = device_index % 2 ** (depth_step + 1) == 2**depth_step - 1
         keep_left = jnp.where(owner, left_gram, keep_left)
         keep_right = jnp.where(owner, right_gram, keep_right)
-        owned = jnp.logical_or(owned, owner)
         current = left_gram + right_gram
     all_grams = jnp.concatenate(
         [
@@ -88,21 +200,7 @@
         ],
         axis=0,
     )
-    all_lower = jnp.linalg.cholesky(all_grams)
-    all_upper = jnp.swapaxes(all_lower, 1, 2)
-    leaf_basis = lax.linalg.triangular_solve(
-        all_lower[0:4], own_rows, left_side=False, lower=True, transpose_a=True
-    )
-    left_parts = jnp.stack([all_upper[0], all_upper[2], all_upper[4], all_upper[7]], axis=0)
-    right_parts = jnp.stack([all_upper[1], all_upper[3], all_upper[5], all_upper[8]], axis=0)
-    parent_lower = jnp.stack([all_lower[4], all_lower[5], all_lower[6], all_lower[9]], axis=0)
-    stacked_rows = jnp.concatenate([left_parts, right_parts], axis=1)
-    node_transfer = lax.linalg.triangular_solve(
-        parent_lower, stacked_rows, left_side=False, lower=True, transpose_a=True
-    )
-    kept = jnp.where(owned, node_transfer[3], jnp.zeros_like(node_transfer[3]))
-    transfer = jnp.stack([node_transfer[0], node_transfer[1], node_transfer[2], kept], axis=0)
-    return (leaf_basis, transfer)
+    return factor(all_grams, own_rows)
 
 
 def solution(mesh):

time: 426 us -> 221 us (0.52); the launches traced: 420 us -> 220 us
  other arithmetic: 200 us -> 2.47 us
  matrix products: 52.2 us -> 36 us
  Pallas kernels: 0 us -> 14.7 us
    another operation x10 -> x0, other arithmetic: 197 us -> none  [the longest x4 118 us: on_device(): all_lower = jnp.linalg.cholesky(all_grams)]
    pallas_call x0 -> x1, Pallas kernels: none -> 14.7 us  [factor(): pl.pallas_call(factor_kernel, out_shape=(jax.ShapeDtypeStruct((4, 64, 128...]
    dot_general x1, matrix products: 31.4 us -> 22.2 us  [on_device(): jnp.einsum('bik,bip->bkp', v_flat, whole_probe[col_flat], precision=fast)]
    dot_general x1, matrix products: 18.2 us -> 13.2 us  [on_device(): jnp.einsum('cbik,cbkp->cip', masked_rows, coeff.reshape(n_local, n_blocks...]
where the time goes in v1:
time: 221 us; the launch traced here: 220 us
  waiting for transfers between devices  88.4 us (40%)
  matrix products  36 us (16%)
  blocking collectives  31.2 us (14%)
  local copies, waits for them, and re-layouts  25 us (11%)
  Pallas kernels  14.7 us (7%)
  between operations  14.2 us (6%)
  starting transfers between devices  8.49 us (4%)
  other arithmetic  2.47 us (1%)
    all_gather x1, waiting for transfers between devices, on_device(): whole_probe = lax.all_gather(omega, 'dev', axis=1, tiled=True)[0]  74.5 us
    gather x1, local copies, waits for them, and re-layouts, on_device(): whole_probe[col_flat]  23.4 us
    dot_general x1, matrix products, on_device(): jnp.einsum('bik,bip->bkp', v_flat, whole_probe[col_flat], precision=fast)  22.2 us
    all_to_all x1, blocking collectives, copy_for_each(): return lax.all_to_all(copies, axis, split_axis=0, concat_axis=0, tiled=True)  17.1 us
    pallas_call x1, Pallas kernels, factor(): pl.pallas_call(factor_kernel, out_shape=(jax.ShapeDtypeStruct((4, 64, 128...  14.7 us
    all_to_all x1, blocking collectives, sum_at_owner(): lax.all_to_all(pieces, axis, split_axis=0, concat_axis=0, tiled=True)  14.1 us
    ppermute x5, waiting for transfers between devices, swapped(): return lax.ppermute(value, axis, pairs)  13.2 us
    dot_general x1, matrix products, on_device(): jnp.einsum('cbik,cbkp->cip', masked_rows, coeff.reshape(n_local, n_blocks...  13.2 us
  transfers between devices with their start and end apart: 6, of which 6 were waited for; matrix products, arithmetic and copies ran while one was open for 1% of the time, Pallas kernels for 0%

profile of v1, /device:TPU:0, one launch (start us, length us, event | category | flops | bytes accessed | tf_op | source)
XLA Modules:
  0.0 220.5 jit_solution(5452580676246140754)
XLA Ops:
  7.2 0.0 all-gather.2.cloned.1.call-start
  7.2 0.7 all-gather.2.cloned.1.call-update
  7.9 0.5 broadcast.42
  8.4 1.3 reduce.5
  9.8 0.1 reshape_squeeze.6
  9.9 0.8 fusion.2
  10.7 74.5 %all-gather.2.cloned.1.call-done = f32[1,128,256,128]{3,2,0,1:T(8,128)} async-done(((f32[1,4,256,128]{3,2,0,1:T(8,128)}), f32[1,128,256,128]{3,2,0,1:T(8,128)}) %all-gather.2.cloned.1.call-update) | async-done | bytes 16777232 | tf_op jit(solution)/shard_map/all_gather | solution.py:160
  85.2 23.4 %gather_fusion = f32[320,256,128]{2,1,0:T(8,128)} fusion(f32[128,256,128]{2,1,0:T(8,128)} %bitcast.31, s32[1024]{0:T(1024)S(1)} %pad_clamp_fusion), kind=kCustom, calls=%fused_computation | custom fusion | bytes 83887360 | tf_op jit(solution)/shard_map/gather | solution.py:161
  108.6 22.2 %fusion.20 = f32[320,128,32]{1,2,0:T(8,128)} fusion(f32[320,256,128]{2,1,0:T(8,128)} %gather_fusion, f32[320,256,32]{1,2,0:T(8,128)} %bitcast.32), kind=kOutput, calls=%fused_computation.42 | convolution fusion | flops 2013265920 | bytes 57671680 | tf_op jit(solution)/shard_map/bik,bip->bkp/dot_general | solution.py:161
  130.7 13.2 %fusion = f32[4,256,128,1]{2,1,3,0:T(8,128)S(1)} fusion(f32[4,80,32,128]{3,2,1,0:T(8,128)} %bitcast.33, f32[1,4,80,256,32]{3,4,2,1,0:T(8,128)} %param.6, f32[4,80,32]{2,1,0:T(8,128)S(1)} %fusion.2), kind=kOutput, calls=%fused_computation.2 | convolution fusion | flops 2015887360 | bytes 16293888 | tf_op jit(solution)/shard_map/cbik,cbkp->cip/dot_general | solution.py:166
  144.0 14.1 %all_to_all.10 = f32[4,4,64,128]{3,2,1,0:T(8,128)S(1)} all-to-all(f32[4,4,64,128]{3,2,1,0:T(8,128)S(1)} %bitcast.34), channel_id=1, replica_groups=mesh['grp'=4,'dev'=32] {'grp'}, dimensions={0} | all-to-all | bytes 1048576 | tf_op jit(solution)/shard_map/all_to_all | solution.py:132
  158.1 0.0 copy-start
  158.1 0.6 fusion.21
  158.7 0.1 broadcast_in_dim.16
  158.8 17.1 %all_to_all.11 = f32[4,4,128,128]{3,2,1,0:T(8,128)S(1)} all-to-all(f32[4,4,128,128]{3,2,1,0:T(8,128)S(1)} %broadcast_in_dim.16), channel_id=1, replica_groups=mesh['grp'=4,'dev'=32] {'grp'}, dimensions={0} | all-to-all | bytes 2097152 | tf_op jit(solution)/shard_map/all_to_all | solution.py:138
  175.9 0.1 reduce_sum.19
  176.1 0.1 collective-permute-start
  176.2 1.2 collective-permute-done
  177.4 1.5 collective-permute-start.1
  179.0 2.8 %collective-permute-done.1 = f32[128,128]{1,0:T(8,128)S(1)} collective-permute-done((f32[128,128]{1,0:T(8,128)S(1)}, f32[128,128]{1,0:T(8,128)S(1)}, u32[]{:S(2)}, u32[]{:S(2)}) %collective-permute-start.1) | collective-permute-done | bytes 65568 | tf_op jit(solution)/shard_map/ppermute | solution.py:148
  181.8 3.1 %collective-permute-start.2 = (f32[128,128]{1,0:T(8,128)S(1)}, f32[128,128]{1,0:T(8,128)S(1)}, u32[]{:S(2)}, u32[]{:S(2)}) collective-permute-start(f32[128,128]{1,0:T(8,128)S(1)} %fusion.14), channel_id=1, source_target_pairs={{0,4},{1,5},{2,6},{3,7},{4,0},{5,1},{6,2},{7,3},{8,12},{9,13},{10,... | collective-permute-start | bytes 196616 | tf_op jit(solution)/shard_map/ppermute | solution.py:148
  184.9 2.8 %collective-permute-done.2 = f32[128,128]{1,0:T(8,128)S(1)} collective-permute-done((f32[128,128]{1,0:T(8,128)S(1)}, f32[128,128]{1,0:T(8,128)S(1)}, u32[]{:S(2)}, u32[]{:S(2)}) %collective-permute-start.2) | collective-permute-done | bytes 65568 | tf_op jit(solution)/shard_map/ppermute | solution.py:148
  187.7 1.1 collective-permute-start.3
  188.8 3.2 %collective-permute-done.3 = f32[128,128]{1,0:T(8,128)S(1)} collective-permute-done((f32[128,128]{1,0:T(8,128)S(1)}, f32[128,128]{1,0:T(8,128)S(1)}, u32[]{:S(2)}, u32[]{:S(2)}) %collective-permute-start.3) | collective-permute-done | bytes 65568 | tf_op jit(solution)/shard_map/ppermute | solution.py:148
  192.0 2.6 %collective-permute-start.4 = (f32[128,128]{1,0:T(8,128)S(1)}, f32[128,128]{1,0:T(8,128)S(1)}, u32[]{:S(2)}, u32[]{:S(2)}) collective-permute-start(f32[128,128]{1,0:T(8,128)S(1)} %fusion.12), channel_id=1, source_target_pairs={{0,16},{1,17},{2,18},{3,19},{4,20},{5,21},{6,22},{7,23},{8,24},{9,... | collective-permute-start | bytes 196616 | tf_op jit(solution)/shard_map/ppermute | solution.py:148
  194.7 3.2 %collective-permute-done.4 = f32[128,128]{1,0:T(8,128)S(1)} collective-permute-done((f32[128,128]{1,0:T(8,128)S(1)}, f32[128,128]{1,0:T(8,128)S(1)}, u32[]{:S(2)}, u32[]{:S(2)}) %collective-permute-start.4) | collective-permute-done | bytes 65568 | tf_op jit(solution)/shard_map/ppermute | solution.py:148
  197.9 0.1 bitcast_dynamic-update-slice_fusion.1
  198.0 0.0 copy-done
  198.0 0.0 copy-start.1
  198.0 0.8 copy-done.1
  198.9 14.7 %factor.1 = (f32[4,64,128]{2,1,0:T(8,128)}, f32[4,256,128]{2,1,0:T(8,128)}) custom-call(f32[10,128,128]{2,1,0:T(8,128)} %copy-done.1, f32[4,64,128]{2,1,0:T(8,128)} %copy-done), custom_call_target="tpu_custom_call" | custom-call | tf_op jit(solution)/shard_map/factor/pallas_call | solution.py:111
  (13 shorter events, 0.3 us)
Async XLA Ops:
  7.2 78.0 %all-gather.2.cloned.1.call-start = ((), (), s32[]{:S(2)}) async-start(), calls=%async_computation.2 | async-start | bytes 17301504 | tf_op jit(solution)/shard_map/all_gather | solution.py:160
  158.1 39.9 %copy-start = (f32[4,64,128]{2,1,0:T(8,128)}, f32[4,64,128]{2,1,0:T(8,128)S(1)}, u32[]{:S(2)}) copy-start(f32[4,64,128]{2,1,0:T(8,128)S(1)} %reduce_sum.18.rows_ref) | copy-start | bytes 393220
  176.1 1.3 collective-permute-start
  177.4 4.3 %collective-permute-start.1 = (f32[128,128]{1,0:T(8,128)S(1)}, f32[128,128]{1,0:T(8,128)S(1)}, u32[]{:S(2)}, u32[]{:S(2)}) collective-permute-start(f32[128,128]{1,0:T(8,128)S(1)} %fusion.11), channel_id=1, source_target_pairs={{0,2},{1,3},{2,0},{3,1},{4,6},{5,7},{6,4},{7,5},{8,10},{9,11},{10,... | collective-permute-start | bytes 196616 | tf_op jit(solution)/shard_map/ppermute | solution.py:148
  181.8 5.8 %collective-permute-start.2 = (f32[128,128]{1,0:T(8,128)S(1)}, f32[128,128]{1,0:T(8,128)S(1)}, u32[]{:S(2)}, u32[]{:S(2)}) collective-permute-start(f32[128,128]{1,0:T(8,128)S(1)} %fusion.14), channel_id=1, source_target_pairs={{0,4},{1,5},{2,6},{3,7},{4,0},{5,1},{6,2},{7,3},{8,12},{9,13},{10,... | collective-permute-start | bytes 196616 | tf_op jit(solution)/shard_map/ppermute | solution.py:148
  187.7 4.3 %collective-permute-start.3 = (f32[128,128]{1,0:T(8,128)S(1)}, f32[128,128]{1,0:T(8,128)S(1)}, u32[]{:S(2)}, u32[]{:S(2)}) collective-permute-start(f32[128,128]{1,0:T(8,128)S(1)} %fusion.13), channel_id=1, source_target_pairs={{0,8},{1,9},{2,10},{3,11},{4,12},{5,13},{6,14},{7,15},{8,0},{9,1},... | collective-permute-start | bytes 196616 | tf_op jit(solution)/shard_map/ppermute | solution.py:148
  192.0 5.8 %collective-permute-start.4 = (f32[128,128]{1,0:T(8,128)S(1)}, f32[128,128]{1,0:T(8,128)S(1)}, u32[]{:S(2)}, u32[]{:S(2)}) collective-permute-start(f32[128,128]{1,0:T(8,128)S(1)} %fusion.12), channel_id=1, source_target_pairs={{0,16},{1,17},{2,18},{3,19},{4,20},{5,21},{6,22},{7,23},{8,24},{9,... | collective-permute-start | bytes 196616 | tf_op jit(solution)/shard_map/ppermute | solution.py:148
  198.0 0.8 copy-start.1
Sparse Core Ops, SparseCore 0:
  10.2 74.8 all-gather.1

commit v2 on v1

--- a/solution.py
+++ b/solution.py
@@ -121,6 +121,211 @@
     )(grams, rows)
 
 
+RIGHT, LEFT, DOWN, UP, ACROSS = range(5)
+
+
+def split_two(x):
+    high = x.astype(jnp.bfloat16)
+    low = (x - high.astype(jnp.float32)).astype(jnp.bfloat16)
+    return high, low
+
+
+def bf16_dot(x, y):
+    return lax.dot_general(x, y, (((1,), (0,)), ((), ())), preferred_element_type=jnp.float32)
+
+
+def gather_kernel(
+    slot_ref, place_ref, rank_ref, omega_ref, u_ref, v_ref, sketch_ref,
+    probe, u_all, v_all, u_high, u_low, coeff, weights, load_sem, send_sem, recv_sem,
+):
+    me = lax.axis_index("dev")
+    core = me % 2
+    x_at = me // 2 % 4
+    y_at = me // 8
+    partner = me + 1 - 2 * core
+
+    def device(dy, dx):
+        return ((y_at + dy) % 4 * 4 + (x_at + dx) % 4) * 2 + core
+
+    targets = (device(0, 1), device(0, 3), device(1, 0), device(3, 0), partner)
+    own = pltpu.make_async_copy(omega_ref, probe.at[pl.ds(me * 4, 4)], load_sem.at[0])
+    own.start()
+    loads = [
+        pltpu.make_async_copy(v_ref, v_all, load_sem.at[1]),
+        pltpu.make_async_copy(u_ref, u_all, load_sem.at[2]),
+    ]
+    for load in loads:
+        load.start()
+    barrier = pltpu.get_barrier_semaphore()
+    for target in targets:
+        pl.semaphore_signal(barrier, inc=1, device_id={"dev": target}, device_id_type=pl.DeviceIdType.MESH)
+    pl.semaphore_wait(barrier, 5)
+    own.wait()
+
+    def move(cluster, way):
+        return pltpu.make_async_remote_copy(
+            src_ref=probe.at[cluster],
+            dst_ref=probe.at[cluster],
+            send_sem=send_sem.at[way],
+            recv_sem=recv_sem.at[cluster],
+            device_id={"dev": targets[way]},
+            device_id_type=pl.DeviceIdType.MESH,
+        )
+
+    def await_cluster(cluster):
+        move(cluster, RIGHT).wait_recv()
+
+    def make_coeff(cluster):
+        wide = jnp.concatenate(split_two(probe[cluster]), axis=1)
+        rows = jnp.concatenate([v_all[slot_ref[cluster * 3 + t]] for t in range(3)], axis=0)
+        high, low = split_two(rows)
+        both = bf16_dot(high, wide)
+        made = both[:, 0:128] + both[:, 128:256] + bf16_dot(low, wide[:, 0:128])
+        packed = jnp.concatenate(split_two(made), axis=1)
+        for t in range(3):
+            coeff[cluster * 3 + t] = packed[t * 32 : t * 32 + 32]
+
+    rank_row = lax.broadcasted_iota(jnp.int32, (32, 256), 0)
+
+    def turn_rows(chunk):
+        pieces = [
+            jnp.where(rank_row < rank_ref[chunk * 8 + e], u_all[chunk * 8 + e], 0.0) for e in range(8)
+        ]
+        high, low = split_two(jnp.concatenate(pieces, axis=0).T)
+        leaf = chunk // 10
+        where = pl.ds(pl.multiple_of(chunk % 10 * 256, 256), 256)
+        u_high[leaf, :, where] = high
+        u_low[leaf, :, where] = low
+
+    def step(dy, dx, j, before, first=False, chunk=None):
+        along_x = device(dy, dx) * 4 + j
+        along_y = device(dx, dy) * 4 + j + 2
+        flips = ((along_x, (RIGHT, LEFT, DOWN, UP)), (along_y, (DOWN, UP, RIGHT, LEFT)))
+        for cluster, (ahead, back, out, home) in flips:
+            if not first:
+                await_cluster(cluster)
+            ways = []
+            if isinstance(dy, int) and dy == 0:
+                if first:
+                    ways += [ahead, back]
+                elif dx == 3 and j == 0:
+                    ways += [ahead]
+                elif dx == 1 and j == 1:
+                    ways += [back]
+                ways += [out, home]
+            elif dy == 3 and j == 0:
+                ways += [out]
+            elif dy == 1 and j == 1:
+                ways += [home]
+            for way in ways + [ACROSS]:
+                move(cluster, way).start()
+        now = [along_x, along_y]
+        work = list(now)
+        if before is not None:
+            for cluster in before:
+                await_cluster(cluster)
+                work.append(cluster)
+        if first and j == 0:
+            loads[0].wait()
+        for cluster in work:
+            make_coeff(cluster)
+        if chunk is not None:
+            turn_rows(chunk)
+            turn_rows(chunk + 1)
+        shift = 4 - 8 * core
+        return [c + shift for c in now]
+
+    late = step(0, 0, 0, None, first=True)
+    late = step(0, 0, 1, late, first=True)
+    loads[1].wait()
+
+    def turn_some(chunk, carry):
+        turn_rows(chunk)
+        return carry
+
+    lax.fori_loop(0, 8, turn_some, 0)
+    for dx, j in ((3, 0), (1, 1), (3, 1), (1, 0), (2, 0), (2, 1)):
+        late = step(0, dx, j, late)
+
+    def far(q):
+        return jnp.where(q == 0, 0, jnp.where(q == 1, 3, q - 1))
+
+    def cross(q, late):
+        for s, (dy, j) in enumerate(((3, 0), (1, 1), (3, 1), (1, 0))):
+            late = step(dy, far(q), j, late, chunk=8 + q * 8 + s * 2)
+        return tuple(late)
+
+    def end(q, late):
+        for j in range(2):
+            late = step(2, far(q), j, late)
+        return tuple(late)
+
+    late = lax.fori_loop(0, 4, cross, tuple(late))
+    late = lax.fori_loop(0, 4, end, late)
+    for cluster in late:
+        await_cluster(cluster)
+    for cluster in late:
+        make_coeff(cluster)
+
+    def sketch_leaf(leaf, carry):
+        for b in range(80):
+            weights[b * 32 : b * 32 + 32, :] = coeff[place_ref[leaf * 80 + b]]
+        both = bf16_dot(u_high[leaf], weights[...])
+        sketch_ref[leaf] = both[:, 0:128] + both[:, 128:256] + bf16_dot(u_low[leaf], weights[:, 0:128])
+        return carry
+
+    lax.fori_loop(0, 4, sketch_leaf, 0)
+    for way in range(4):
+        span = pl.ds(0, 15)
+        pltpu.make_async_remote_copy(
+            src_ref=probe.at[span], dst_ref=probe.at[span], send_sem=send_sem.at[way], recv_sem=recv_sem.at[0],
+            device_id={"dev": targets[way]}, device_id_type=pl.DeviceIdType.MESH,
+        ).wait_send()
+    span = pl.ds(0, 64)
+    pltpu.make_async_remote_copy(
+        src_ref=probe.at[span], dst_ref=probe.at[span], send_sem=send_sem.at[ACROSS], recv_sem=recv_sem.at[0],
+        device_id={"dev": partner}, device_id_type=pl.DeviceIdType.MESH,
+    ).wait_send()
+
+
+def sketch_of_group(slots, places, ranks, omega, u_rows, v_rows):
+    smem = pl.BlockSpec(memory_space=pltpu.SMEM)
+    anywhere = pl.BlockSpec(memory_space=pl.ANY)
+    return pl.pallas_call(
+        gather_kernel,
+        out_shape=jax.ShapeDtypeStruct((4, 256, 128), jnp.float32),
+        in_specs=[smem, smem, smem, anywhere, anywhere, anywhere],
+        out_specs=pl.BlockSpec(memory_space=pltpu.VMEM),
+        scratch_shapes=[
+            pltpu.VMEM((128, 256, 128), jnp.float32),
+            pltpu.VMEM((320, 32, 256), jnp.float32),
+            pltpu.VMEM((320, 32, 256), jnp.float32),
+            pltpu.VMEM((4, 256, 2560), jnp.bfloat16),
+            pltpu.VMEM((4, 256, 2560), jnp.bfloat16),
+            pltpu.VMEM((384, 32, 256), jnp.bfloat16),
+            pltpu.VMEM((2560, 256), jnp.bfloat16),
+            pltpu.SemaphoreType.DMA((3,)),
+            pltpu.SemaphoreType.DMA((5,)),
+            pltpu.SemaphoreType.DMA((128,)),
+        ],
+        compiler_params=pltpu.CompilerParams(
+            collective_id=0, has_side_effects=True, vmem_limit_bytes=62 * 2**20
+        ),
+        name="gather",
+    )(slots, places, ranks, omega, u_rows, v_rows)
+
+
+def sort_blocks(columns):
+    named = columns[0, :, :, 0].reshape(320)
+    number = jnp.arange(320, dtype=jnp.int32)
+    same = named[:, None] == named[None, :]
+    turn = jnp.sum((same & (number[None, :] < number[:, None])).astype(jnp.int32), axis=1)
+    places = named * 3 + turn
+    slots = jnp.arange(384, dtype=jnp.int32)
+    hit = places[None, :] == slots[:, None]
+    return jnp.sum(jnp.where(hit, number[None, :], 0), axis=1), places
+
+
 def split_up(value, dim, count):
     dims = value.shape
     pieces = value.reshape(*dims[:dim], count, dims[dim] // count, *dims[dim + 1 :])
@@ -149,26 +354,12 @@
 
 
 def on_device(omega, u_factor, v_factor, columns, ranks):
-    n_local = u_factor.shape[1]
-    n_blocks = u_factor.shape[2]
-    leaf_rows = u_factor.shape[3]
-    rank_width = u_factor.shape[4]
     probe_count = omega.shape[3]
     dev_count = lax.axis_size("dev")
-    col_flat = columns[0, :, :, 0].reshape(n_local * n_blocks)
-    v_flat = v_factor[0].reshape(n_local * n_blocks, leaf_rows, rank_width)
-    whole_probe = lax.all_gather(omega, "dev", axis=1, tiled=True)[0]
-    coeff = jnp.einsum("bik,bip->bkp", v_flat, whole_probe[col_flat], precision=fast)
-    rank_mask = (
-        jnp.arange(rank_width, dtype=jnp.int32)[None, None, :] < ranks[0][:, :, None]
-    ).astype(jnp.float32)
-    masked_rows = u_factor[0] * rank_mask[:, :, None, :]
-    partial_sketch = jnp.einsum(
-        "cbik,cbkp->cip",
-        masked_rows,
-        coeff.reshape(n_local, n_blocks, rank_width, probe_count),
-        precision=fast,
-    )
+    slots, places = sort_blocks(columns)
+    u_rows = jnp.swapaxes(u_factor, 3, 4).reshape(320, 32, 256)
+    v_rows = jnp.swapaxes(v_factor, 3, 4).reshape(320, 32, 256)
+    partial_sketch = sketch_of_group(slots, places, ranks.reshape(320), omega[0], u_rows, v_rows)
     own_rows = sum_at_owner(partial_sketch, "grp", 1)
     gram_matrix = taken_together(
         jnp.einsum("cip,ciq->cpq", own_rows, own_rows, precision=precise), "grp"

time: 221 us -> 134 us (0.61)
  waiting for transfers between devices: 88.4 us -> 18.9 us
  Pallas kernels: 14.7 us -> 71.1 us
  matrix products: 36 us -> 0.59 us
  local copies, waits for them, and re-layouts: 25 us -> 3.99 us
  between operations: 14.2 us -> 0.79 us
  starting transfers between devices: 8.49 us -> 3.28 us
    all_gather x1 -> x0, waiting for transfers between devices: 74.5 us -> none  [on_device(): whole_probe = lax.all_gather(omega, 'dev', axis=1, tiled=True)[0]]
    pallas_call x0 -> x1, Pallas kernels: none -> 56.4 us  [sketch_of_group(): pl.pallas_call(gather_kernel, out_shape=jax.ShapeDtypeStruct((4, 256, 128...]
    dot_general x2 -> x0, matrix products: 35.4 us -> none  [the longest x1 22.2 us: on_device(): jnp.einsum('bik,bip->bkp', v_flat, whole_probe[col_flat], precision=fast)]
    gather x1 -> x0, local copies, waits for them, and re-layouts: 23.4 us -> none  [on_device(): whole_probe[col_flat]]
    ppermute x5, waiting for transfers between devices: 13.2 us -> 18.9 us  [swapped(): return lax.ppermute(value, axis, pairs)]
    ppermute x5, starting transfers between devices: 8.45 us -> 3.28 us  [swapped(): return lax.ppermute(value, axis, pairs)]
  transfers between devices with their start and end apart: 6 -> 5, of which waited for: 6 -> 5; matrix products, arithmetic and copies ran while one was open for 1% -> 0% of each run, Pallas kernels for 0% -> 0%
where the time goes in v2:
time: 134 us
  Pallas kernels  71.1 us (53%)
  blocking collectives  32.3 us (24%)
  waiting for transfers between devices  18.9 us (14%)
  local copies, waits for them, and re-layouts  3.99 us (3%)
  starting transfers between devices  3.28 us (2%)
  other arithmetic  2.59 us (2%)
    pallas_call x1, Pallas kernels, sketch_of_group(): pl.pallas_call(gather_kernel, out_shape=jax.ShapeDtypeStruct((4, 256, 128...  56.4 us
    ppermute x5, waiting for transfers between devices, swapped(): return lax.ppermute(value, axis, pairs)  18.9 us
    all_to_all x1, blocking collectives, copy_for_each(): return lax.all_to_all(copies, axis, split_axis=0, concat_axis=0, tiled=True)  17.2 us
    all_to_all x1, blocking collectives, sum_at_owner(): lax.all_to_all(pieces, axis, split_axis=0, concat_axis=0, tiled=True)  15.1 us
    pallas_call x1, Pallas kernels, factor(): pl.pallas_call(factor_kernel, out_shape=(jax.ShapeDtypeStruct((4, 64, 128...  14.7 us
    ppermute x5, starting transfers between devices, swapped(): return lax.ppermute(value, axis, pairs)  3.28 us
  transfers between devices with their start and end apart: 5, of which 5 were waited for; matrix products, arithmetic and copies ran while one was open for 0% of the time, Pallas kernels for 0%

profile of v2, /device:TPU:0, one launch (start us, length us, event | category | flops | bytes accessed | tf_op | source)
XLA Modules:
  0.0 133.6 jit_solution(2011715183383768788)
XLA Ops:
  0.6 0.5 broadcast.22
  1.1 1.3 %reduce.3 = s32[4,80]{1,0:T(4,128)S(1)} reduce(s32[1,4,80,1]{2,3,1,0:T(1,128)} %param.8, s32[]{:T(128)} %broadcast.22), dimensions={0,3}, to_apply=%param.8.reduce_sub_computation.3 | reduce | bytes 2564 | tf_op args[3]
  2.5 0.1 reshape_squeeze.3
  2.6 0.2 convert_reduce_fusion
  2.8 0.0 copy-start.2
  2.8 0.7 select_reduce_fusion.slot_ref
  3.5 1.4 %reshape.27.rank_ref = s32[320]{0:T(512)} reshape(s32[1,4,80]{2,1,0:T(4,128)} %param.9) | data formatting | bytes 2560 | tf_op jit(solution)/shard_map/reshape | solution.py:362
  4.9 0.0 copy-done.2
  4.9 56.4 %gather.1 = f32[4,256,128]{2,1,0:T(8,128)} custom-call(s32[384]{0:T(512)} %select_reduce_fusion.slot_ref, s32[320]{0:T(512)} %copy-done.2, s32[320]{0:T(512)} %reshape.27.rank_ref, f32[4,256,128]{2,1,0:T(8,128)} %bitcast.26, f32[320,32,256]{2,1,0:T(8,128)} %bitcast.22, f32[320,32,256]{2,1,0:T(8,128)} %bitcast.23), custom_call_target="tpu_custom_call" | custom-call | tf_op jit(solution)/shard_map/gather/pallas_call | solution.py:294
  61.3 1.1 copy.10
  62.3 15.1 %all_to_all.10 = f32[4,4,64,128]{3,2,1,0:T(8,128)S(1)} all-to-all(f32[4,4,64,128]{3,2,1,0:T(8,128)S(1)} %bitcast.25), channel_id=1, replica_groups=mesh['grp'=4,'dev'=32] {'grp'}, dimensions={0} | all-to-all | bytes 1048576 | tf_op jit(solution)/shard_map/all_to_all | solution.py:337
  77.5 0.0 copy-start
  77.5 0.6 fusion.17
  78.1 0.1 broadcast_in_dim.32
  78.2 17.2 %all_to_all.11 = f32[4,4,128,128]{3,2,1,0:T(8,128)S(1)} all-to-all(f32[4,4,128,128]{3,2,1,0:T(8,128)S(1)} %broadcast_in_dim.32), channel_id=1, replica_groups=mesh['grp'=4,'dev'=32] {'grp'}, dimensions={0} | all-to-all | bytes 2097152 | tf_op jit(solution)/shard_map/all_to_all | solution.py:343
  95.4 0.1 reduce_sum.39
  95.6 0.1 collective-permute-start
  95.7 1.2 collective-permute-done
  96.9 0.3 collective-permute-start.1
  97.2 4.0 %collective-permute-done.1 = f32[128,128]{1,0:T(8,128)S(1)} collective-permute-done((f32[128,128]{1,0:T(8,128)S(1)}, f32[128,128]{1,0:T(8,128)S(1)}, u32[]{:S(2)}, u32[]{:S(2)}) %collective-permute-start.1) | collective-permute-done | bytes 65568 | tf_op jit(solution)/shard_map/ppermute | solution.py:353
  101.3 1.8 %collective-permute-start.2 = (f32[128,128]{1,0:T(8,128)S(1)}, f32[128,128]{1,0:T(8,128)S(1)}, u32[]{:S(2)}, u32[]{:S(2)}) collective-permute-start(f32[128,128]{1,0:T(8,128)S(1)} %fusion.12), channel_id=1, source_target_pairs={{0,4},{1,5},{2,6},{3,7},{4,0},{5,1},{6,2},{7,3},{8,12},{9,13},{10,... | collective-permute-start | bytes 196616 | tf_op jit(solution)/shard_map/ppermute | solution.py:353
  103.0 4.1 %collective-permute-done.2 = f32[128,128]{1,0:T(8,128)S(1)} collective-permute-done((f32[128,128]{1,0:T(8,128)S(1)}, f32[128,128]{1,0:T(8,128)S(1)}, u32[]{:S(2)}, u32[]{:S(2)}) %collective-permute-start.2) | collective-permute-done | bytes 65568 | tf_op jit(solution)/shard_map/ppermute | solution.py:353
  107.1 0.1 collective-permute-start.3
  107.3 4.7 %collective-permute-done.3 = f32[128,128]{1,0:T(8,128)S(1)} collective-permute-done((f32[128,128]{1,0:T(8,128)S(1)}, f32[128,128]{1,0:T(8,128)S(1)}, u32[]{:S(2)}, u32[]{:S(2)}) %collective-permute-start.3) | collective-permute-done | bytes 65568 | tf_op jit(solution)/shard_map/ppermute | solution.py:353
  112.0 1.0 collective-permute-start.4
  113.0 4.8 %collective-permute-done.4 = f32[128,128]{1,0:T(8,128)S(1)} collective-permute-done((f32[128,128]{1,0:T(8,128)S(1)}, f32[128,128]{1,0:T(8,128)S(1)}, u32[]{:S(2)}, u32[]{:S(2)}) %collective-permute-start.4) | collective-permute-done | bytes 65568 | tf_op jit(solution)/shard_map/ppermute | solution.py:353
  117.9 0.1 bitcast_dynamic-update-slice_fusion.1
  118.0 0.0 copy-done
  118.0 0.0 copy-start.1
  118.0 0.8 copy-done.1
  118.8 14.7 %factor.1 = (f32[4,64,128]{2,1,0:T(8,128)}, f32[4,256,128]{2,1,0:T(8,128)}) custom-call(f32[10,128,128]{2,1,0:T(8,128)} %copy-done.1, f32[4,64,128]{2,1,0:T(8,128)} %copy-done), custom_call_target="tpu_custom_call" | custom-call | tf_op jit(solution)/shard_map/factor/pallas_call | solution.py:111
  (11 shorter events, 0.2 us)
Async XLA Ops:
  2.8 2.1 %copy-start.2 = (s32[320]{0:T(512)}, s32[320]{0:T(512)S(1)}, u32[]{:S(2)}) copy-start(s32[320]{0:T(512)S(1)} %multiply_add_fusion.place_ref) | copy-start | bytes 3844
  77.5 40.5 %copy-start = (f32[4,64,128]{2,1,0:T(8,128)}, f32[4,64,128]{2,1,0:T(8,128)S(1)}, u32[]{:S(2)}) copy-start(f32[4,64,128]{2,1,0:T(8,128)S(1)} %reduce_sum.38.rows_ref) | copy-start | bytes 393220
  95.6 1.3 collective-permute-start
  96.9 4.3 %collective-permute-start.1 = (f32[128,128]{1,0:T(8,128)S(1)}, f32[128,128]{1,0:T(8,128)S(1)}, u32[]{:S(2)}, u32[]{:S(2)}) collective-permute-start(f32[128,128]{1,0:T(8,128)S(1)} %fusion.9), channel_id=1, source_target_pairs={{0,2},{1,3},{2,0},{3,1},{4,6},{5,7},{6,4},{7,5},{8,10},{9,11},{10,... | collective-permute-start | bytes 196616 | tf_op jit(solution)/shard_map/ppermute | solution.py:353
  101.3 5.8 %collective-permute-start.2 = (f32[128,128]{1,0:T(8,128)S(1)}, f32[128,128]{1,0:T(8,128)S(1)}, u32[]{:S(2)}, u32[]{:S(2)}) collective-permute-start(f32[128,128]{1,0:T(8,128)S(1)} %fusion.12), channel_id=1, source_target_pairs={{0,4},{1,5},{2,6},{3,7},{4,0},{5,1},{6,2},{7,3},{8,12},{9,13},{10,... | collective-permute-start | bytes 196616 | tf_op jit(solution)/shard_map/ppermute | solution.py:353
  107.1 4.8 %collective-permute-start.3 = (f32[128,128]{1,0:T(8,128)S(1)}, f32[128,128]{1,0:T(8,128)S(1)}, u32[]{:S(2)}, u32[]{:S(2)}) collective-permute-start(f32[128,128]{1,0:T(8,128)S(1)} %fusion.11), channel_id=1, source_target_pairs={{0,8},{1,9},{2,10},{3,11},{4,12},{5,13},{6,14},{7,15},{8,0},{9,1},... | collective-permute-start | bytes 196616 | tf_op jit(solution)/shard_map/ppermute | solution.py:353
  112.0 5.8 %collective-permute-start.4 = (f32[128,128]{1,0:T(8,128)S(1)}, f32[128,128]{1,0:T(8,128)S(1)}, u32[]{:S(2)}, u32[]{:S(2)}) collective-permute-start(f32[128,128]{1,0:T(8,128)S(1)} %fusion.10), channel_id=1, source_target_pairs={{0,16},{1,17},{2,18},{3,19},{4,20},{5,21},{6,22},{7,23},{8,24},{9,... | collective-permute-start | bytes 196616 | tf_op jit(solution)/shard_map/ppermute | solution.py:353
  118.0 0.8 copy-start.1

commit v3 on v2

--- a/solution.py
+++ b/solution.py
@@ -7,7 +7,6 @@
 from jax.sharding import PartitionSpec as P
 
 precise = lax.Precision.HIGHEST
-fast = lax.Precision.HIGH
 
 
 GROUP = 5
@@ -135,8 +134,10 @@
 
 
 def gather_kernel(
-    slot_ref, place_ref, rank_ref, omega_ref, u_ref, v_ref, sketch_ref,
-    probe, u_all, v_all, u_high, u_low, coeff, weights, load_sem, send_sem, recv_sem,
+    slot_ref, place_ref, rank_ref, omega_ref, u_ref, v_ref, gram_ref, rows_ref,
+    probe, u_all, v_all, u_high, u_low, coeff, weights,
+    sketch, relay, parts, whole, leaf_gram, leaf_rows, top_gram, tree, eights,
+    load_sem, send_sem, recv_sem, out_sem, in_sem,
 ):
     me = lax.axis_index("dev")
     core = me % 2
@@ -156,10 +157,15 @@
     ]
     for load in loads:
         load.start()
+    z = lax.axis_index("grp")
+    e = me % 8
     barrier = pltpu.get_barrier_semaphore()
-    for target in targets:
-        pl.semaphore_signal(barrier, inc=1, device_id={"dev": target}, device_id_type=pl.DeviceIdType.MESH)
-    pl.semaphore_wait(barrier, 5)
+    peers = [{"dev": me // 8 * 8 + (e + n) % 8} for n in range(1, 8)]
+    peers += [{"dev": (me + 8 * n) % 32} for n in range(1, 4)]
+    peers += [{"grp": (z + n) % 4} for n in range(1, 4)]
+    for peer in peers:
+        pl.semaphore_signal(barrier, inc=1, device_id=peer, device_id_type=pl.DeviceIdType.MESH)
+    pl.semaphore_wait(barrier, 13)
     own.wait()
 
     def move(cluster, way):
@@ -267,14 +273,176 @@
     for cluster in late:
         make_coeff(cluster)
 
-    def sketch_leaf(leaf, carry):
+    def sketch_leaf(leaf):
         for b in range(80):
             weights[b * 32 : b * 32 + 32, :] = coeff[place_ref[leaf * 80 + b]]
         both = bf16_dot(u_high[leaf], weights[...])
-        sketch_ref[leaf] = both[:, 0:128] + both[:, 128:256] + bf16_dot(u_low[leaf], weights[:, 0:128])
+        sketch[leaf] = both[:, 0:128] + both[:, 128:256] + bf16_dot(u_low[leaf], weights[:, 0:128])
+
+    def send(source, target, out, arrival, peer):
+        return pltpu.make_async_remote_copy(
+            src_ref=source,
+            dst_ref=target,
+            send_sem=out_sem.at[out],
+            recv_sem=in_sem.at[arrival],
+            device_id=peer,
+            device_id_type=pl.DeviceIdType.MESH,
+        )
+
+    top, bottom = pl.ds(0, 128), pl.ds(128, 128)
+    after, across_z, before = [(z + n) % 4 for n in (1, 2, 3)]
+    to_after, to_across, to_before = [{"grp": n} for n in (after, across_z, before)]
+    far_out = send(sketch.at[across_z, top], relay.at[0], 0, 0, to_after)
+    far_home = send(sketch.at[across_z, bottom], relay.at[1], 1, 1, to_before)
+    near_out = send(sketch.at[after, bottom], parts.at[0], 2, 2, to_after)
+    near_home = send(sketch.at[before, top], parts.at[1], 3, 3, to_before)
+    joint_out = send(sketch.at[after, top], parts.at[2], 4, 4, to_after)
+    joint_home = send(sketch.at[before, bottom], parts.at[3], 5, 5, to_before)
+
+    def leaf_step(n, carry):
+        sketch_leaf((z + jnp.where(n == 0, 2, jnp.where(n == 1, 1, jnp.where(n == 2, 3, 0)))) % 4)
+
+        @pl.when(n == 0)
+        def _():
+            far_out.start()
+            far_home.start()
+
+        @pl.when(n == 1)
+        def _():
+            near_out.start()
+
+        @pl.when(n == 2)
+        def _():
+            near_home.start()
+
         return carry
 
-    lax.fori_loop(0, 4, sketch_leaf, 0)
+    lax.fori_loop(0, 4, leaf_step, 0)
+    far_out.wait_recv()
+    sketch[after, 0:128] = sketch[after, 0:128] + relay[0]
+    joint_out.start()
+    far_home.wait_recv()
+    sketch[before, 128:256] = sketch[before, 128:256] + relay[1]
+    joint_home.start()
+    near_out.wait_recv()
+    near_home.wait_recv()
+    joint_out.wait_recv()
+    whole[0:128] = sketch[z, 0:128] + parts[1] + parts[2]
+    joint_home.wait_recv()
+    whole[128:256] = sketch[z, 128:256] + parts[0] + parts[3]
+    flat = whole[...]
+    leaf_gram[z] = lax.dot_general(
+        flat.T, flat, (((1,), (0,)), ((), ())), precision=precise, preferred_element_type=jnp.float32
+    )
+    others = ((2, across_z, to_across), (1, after, to_after), (3, before, to_before))
+    gram_sends = [send(leaf_gram.at[z], leaf_gram.at[z], 5 + n, 6 + z, peer) for n, _, peer in others]
+    row_sends = [
+        send(whole.at[pl.ds(pl.multiple_of(there * 64, 64), 64)], leaf_rows.at[z], 8 + n, 10 + z, peer)
+        for n, there, peer in others
+    ]
+    for copy in gram_sends + row_sends:
+        copy.start()
+    leaf_rows[z] = whole[pl.ds(pl.multiple_of(z * 64, 64), 64)]
+    for _, there, peer in others:
+        send(leaf_gram.at[there], leaf_gram.at[there], 6, 6 + there, peer).wait_recv()
+    first_pair = leaf_gram[0] + leaf_gram[1]
+    second_pair = leaf_gram[2] + leaf_gram[3]
+    own_top = first_pair + second_pair
+    top_gram[...] = own_top
+
+    def tree_send(slot, target):
+        return send(top_gram, tree.at[e], 12 + slot, 14 + e, {"dev": me // 8 * 8 + target})
+
+    tree_sends = (
+        (e != 7, tree_send(0, 7)),
+        (e != 3, tree_send(1, 3)),
+        (e % 4 != 1, tree_send(2, e // 4 * 4 + 1)),
+        (e % 2 == 1, tree_send(3, e - 1)),
+    )
+    for needed, copy in tree_sends:
+        pl.when(needed)(copy.start)
+    for c in range(4):
+        gram_ref[c] = leaf_gram[c]
+    gram_ref[4] = first_pair
+    gram_ref[5] = second_pair
+    gram_ref[6] = own_top
+
+    def arrived(slot):
+        send(top_gram, tree.at[slot], 12, 14 + slot, to_after).wait_recv()
+        return tree[slot]
+
+    def keep(left, right):
+        gram_ref[7] = left
+        gram_ref[8] = right
+        gram_ref[9] = left + right
+
+    @pl.when(e % 2 == 0)
+    def _():
+        keep(own_top, arrived(e + 1))
+
+    @pl.when(e % 4 == 1)
+    def _():
+        keep(arrived(e - 1) + own_top, arrived(e + 1) + arrived(e + 2))
+
+    @pl.when(e == 3)
+    def _():
+        left = arrived(0) + arrived(1) + (arrived(2) + own_top)
+        keep(left, arrived(4) + arrived(5) + (arrived(6) + arrived(7)))
+
+    def eight_send(slot, row):
+        return send(top_gram, eights.at[y_at], 16 + slot, 22 + y_at, {"dev": row * 8 + 7})
+
+    eight_sends = (
+        (e * 4 + y_at == 28, eight_send(0, 1)),
+        (e * 4 + y_at == 29, eight_send(0, 0)),
+        (e * 4 + y_at == 30, eight_send(0, 1)),
+        (e * 4 + y_at == 31, eight_send(0, 1)),
+        (e * 4 + y_at == 31, eight_send(1, 2)),
+    )
+
+    @pl.when(e == 7)
+    def _():
+        pairs = [arrived(0) + arrived(1), arrived(2) + arrived(3), arrived(4) + arrived(5), arrived(6) + own_top]
+        for needed, copy in tree_sends:
+            pl.when(needed)(copy.wait_send)
+        eight = (pairs[0] + pairs[1]) + (pairs[2] + pairs[3])
+        top_gram[...] = eight
+        for needed, copy in eight_sends:
+            pl.when(needed)(copy.start)
+
+        def landed(row):
+            send(top_gram, eights.at[row], 16, 22 + row, to_after).wait_recv()
+            return eights[row]
+
+        @pl.when(y_at == 0)
+        def _():
+            keep(eight, landed(1))
+
+        @pl.when(y_at == 1)
+        def _():
+            keep(landed(0) + eight, landed(2) + landed(3))
+
+        @pl.when(y_at == 2)
+        def _():
+            keep(eight, landed(3))
+
+        @pl.when(y_at == 3)
+        def _():
+            keep(eight, eight)
+
+        for needed, copy in eight_sends:
+            pl.when(needed)(copy.wait_send)
+
+    @pl.when(e != 7)
+    def _():
+        for needed, copy in tree_sends:
+            pl.when(needed)(copy.wait_send)
+
+    for _, there, peer in others:
+        send(leaf_rows.at[there], leaf_rows.at[there], 9, 10 + there, peer).wait_recv()
+    rows_ref[...] = leaf_rows[...]
+    for copy in [far_out, far_home, near_out, near_home, joint_out, joint_home] + gram_sends + row_sends:
+        copy.wait_send()
     for way in range(4):
         span = pl.ds(0, 15)
         pltpu.make_async_remote_copy(
@@ -288,14 +456,17 @@
     ).wait_send()
 
 
-def sketch_of_group(slots, places, ranks, omega, u_rows, v_rows):
+def sum_sketches(slots, places, ranks, omega, u_rows, v_rows):
     smem = pl.BlockSpec(memory_space=pltpu.SMEM)
     anywhere = pl.BlockSpec(memory_space=pl.ANY)
     return pl.pallas_call(
         gather_kernel,
-        out_shape=jax.ShapeDtypeStruct((4, 256, 128), jnp.float32),
+        out_shape=(
+            jax.ShapeDtypeStruct((10, 128, 128), jnp.float32),
+            jax.ShapeDtypeStruct((4, 64, 128), jnp.float32),
+        ),
         in_specs=[smem, smem, smem, anywhere, anywhere, anywhere],
-        out_specs=pl.BlockSpec(memory_space=pltpu.VMEM),
+        out_specs=(pl.BlockSpec(memory_space=pltpu.VMEM), pl.BlockSpec(memory_space=pltpu.VMEM)),
         scratch_shapes=[
             pltpu.VMEM((128, 256, 128), jnp.float32),
             pltpu.VMEM((320, 32, 256), jnp.float32),
@@ -304,9 +475,20 @@
             pltpu.VMEM((4, 256, 2560), jnp.bfloat16),
             pltpu.VMEM((384, 32, 256), jnp.bfloat16),
             pltpu.VMEM((2560, 256), jnp.bfloat16),
+            pltpu.VMEM((4, 256, 128), jnp.float32),
+            pltpu.VMEM((2, 128, 128), jnp.float32),
+            pltpu.VMEM((4, 128, 128), jnp.float32),
+            pltpu.VMEM((256, 128), jnp.float32),
+            pltpu.VMEM((4, 128, 128), jnp.float32),
+            pltpu.VMEM((4, 64, 128), jnp.float32),
+            pltpu.VMEM((128, 128), jnp.float32),
+            pltpu.VMEM((8, 128, 128), jnp.float32),
+            pltpu.VMEM((4, 128, 128), jnp.float32),
             pltpu.SemaphoreType.DMA((3,)),
             pltpu.SemaphoreType.DMA((5,)),
             pltpu.SemaphoreType.DMA((128,)),
+            pltpu.SemaphoreType.DMA((18,)),
+            pltpu.SemaphoreType.DMA((26,)),
         ],
         compiler_params=pltpu.CompilerParams(
             collective_id=0, has_side_effects=True, vmem_limit_bytes=62 * 2**20
@@ -326,72 +508,12 @@
     return jnp.sum(jnp.where(hit, number[None, :], 0), axis=1), places
 
 
-def split_up(value, dim, count):
-    dims = value.shape
-    pieces = value.reshape(*dims[:dim], count, dims[dim] // count, *dims[dim + 1 :])
-    return jnp.moveaxis(pieces, dim, 0)
-
-
-def sum_at_owner(value, axis, dim):
-    pieces = split_up(value, dim, lax.axis_size(axis))
-    arrived = lax.all_to_all(pieces, axis, split_axis=0, concat_axis=0, tiled=True)
-    return arrived.sum(axis=0)
-
-
-def copy_for_each(value, axis):
-    copies = jnp.broadcast_to(value, (lax.axis_size(axis), *value.shape))
-    return lax.all_to_all(copies, axis, split_axis=0, concat_axis=0, tiled=True)
-
-
-def taken_together(value, axis):
-    return copy_for_each(value, axis).sum(axis=0)
-
-
-def swapped(value, axis, apart):
-    mask = 2**apart
-    pairs = [(source, source ^ mask) for source in range(lax.axis_size(axis))]
-    return lax.ppermute(value, axis, pairs)
-
-
 def on_device(omega, u_factor, v_factor, columns, ranks):
-    probe_count = omega.shape[3]
-    dev_count = lax.axis_size("dev")
     slots, places = sort_blocks(columns)
     u_rows = jnp.swapaxes(u_factor, 3, 4).reshape(320, 32, 256)
     v_rows = jnp.swapaxes(v_factor, 3, 4).reshape(320, 32, 256)
-    partial_sketch = sketch_of_group(slots, places, ranks.reshape(320), omega[0], u_rows, v_rows)
-    own_rows = sum_at_owner(partial_sketch, "grp", 1)
-    gram_matrix = taken_together(
-        jnp.einsum("cip,ciq->cpq", own_rows, own_rows, precision=precise), "grp"
-    )
-    pair_gram = gram_matrix[0::2] + gram_matrix[1::2]
-    top_gram = pair_gram[0] + pair_gram[1]
-    device_index = lax.axis_index("dev")
-    tree_bits = dev_count.bit_length() - 1
-    keep_left = jnp.eye(probe_count, dtype=jnp.float32)
-    keep_right = keep_left
-    current = top_gram
-    for depth_step in range(tree_bits):
-        sibling = swapped(current, "dev", depth_step)
-        is_left = device_index // 2**depth_step % 2 == 0
-        left_gram = jnp.where(is_left, current, sibling)
-        right_gram = jnp.where(is_left, sibling, current)
-        owner = device_index % 2 ** (depth_step + 1) == 2**depth_step - 1
-        keep_left = jnp.where(owner, left_gram, keep_left)
-        keep_right = jnp.where(owner, right_gram, keep_right)
-        current = left_gram + right_gram
-    all_grams = jnp.concatenate(
-        [
-            gram_matrix,
-            pair_gram,
-            top_gram[None],
-            keep_left[None],
-            keep_right[None],
-            (keep_left + keep_right)[None],
-        ],
-        axis=0,
-    )
-    return factor(all_grams, own_rows)
+    grams, rows = sum_sketches(slots, places, ranks.reshape(320), omega[0], u_rows, v_rows)
+    return factor(grams, rows)
 
 
 def solution(mesh):

time: 134 us -> 96.6 us (0.72)
  the two profiles are of different devices: /device:TPU:0 before, /device:TPU:15 now
where the time goes in v3:
time: 96.6 us; the launch traced here: 96.4 us
  Pallas kernels  91.5 us (95%)
  other arithmetic  2.28 us (2%)
  local copies, waits for them, and re-layouts  1.96 us (2%)
    pallas_call x1, Pallas kernels, sum_sketches(): pl.pallas_call(gather_kernel, out_shape=(jax.ShapeDtypeStruct((10, 128, 1...  76.8 us
    pallas_call x1, Pallas kernels, factor(): pl.pallas_call(factor_kernel, out_shape=(jax.ShapeDtypeStruct((4, 64, 128...  14.7 us

profile of v3, /device:TPU:15, one launch (start us, length us, event | category | flops | bytes accessed | tf_op | source)
XLA Modules:
  0.0 96.4 jit_solution(17433418265859999145)
XLA Ops:
  0.6 0.5 broadcast.7
  1.1 1.3 %reduce.3 = s32[4,80]{1,0:T(4,128)S(1)} reduce(s32[1,4,80,1]{2,3,1,0:T(1,128)} %param.8, s32[]{:T(128)} %broadcast.7), dimensions={0,3}, to_apply=%param.8.reduce_sub_computation.3 | reduce | bytes 2564 | tf_op args[3]
  2.5 0.1 reshape_squeeze.3
  2.6 0.2 convert_reduce_fusion
  2.8 0.0 copy-start
  2.8 0.7 select_reduce_fusion.slot_ref
  3.5 1.4 %reshape.23.rank_ref = s32[320]{0:T(512)} reshape(s32[1,4,80]{2,1,0:T(4,128)} %param.9) | data formatting | bytes 2560 | tf_op jit(solution)/shard_map/reshape | solution.py:515
  4.9 0.0 copy-done
  4.9 76.8 %gather.1 = (f32[10,128,128]{2,1,0:T(8,128)}, f32[4,64,128]{2,1,0:T(8,128)}) custom-call(s32[384]{0:T(512)} %select_reduce_fusion.slot_ref, s32[320]{0:T(512)} %copy-done, s32[320]{0:T(512)} %reshape.23.rank_ref, f32[4,256,128]{2,1,0:T(8,128)} %bitcast.10, f32[320,32,256]{2,1,0:T(8,128)} %bitcast.8, f32[320,32,256]{2,1,0:T(8,128)} %bitcast.9), custom_call_target="tpu_custom_call" | custom-call | tf_op jit(solution)/shard_map/gather/pallas_call | solution.py:462
  81.6 14.7 %factor.1 = (f32[4,64,128]{2,1,0:T(8,128)}, f32[4,256,128]{2,1,0:T(8,128)}) custom-call(f32[10,128,128]{2,1,0:T(8,128)} %get-tuple-element.4.gram_ref, f32[4,64,128]{2,1,0:T(8,128)} %get-tuple-element.5.rows_ref), custom_call_target="tpu_custom_call" | custom-call | tf_op jit(solution)/shard_map/factor/pallas_call | solution.py:110
  (1 shorter events, 0.0 us)
Async XLA Ops:
  2.8 2.1 %copy-start = (s32[320]{0:T(512)}, s32[320]{0:T(512)S(1)}, u32[]{:S(2)}) copy-start(s32[320]{0:T(512)S(1)} %multiply_add_fusion.place_ref) | copy-start | bytes 3844

commit v4 on v3

--- a/solution.py
+++ b/solution.py
@@ -16,7 +16,7 @@
     idx = jnp.full(x.shape, lane, jnp.int32)
     return jnp.take_along_axis(x, idx, axis=1)
 
-def factor_all(work, mats):
+def factor_all(work, mats, spans=SEGS):
     sub = lax.broadcasted_iota(jnp.int32, (8, 128), 0)
     lane = lax.broadcasted_iota(jnp.int32, (8, 128), 1)
 
@@ -65,11 +65,12 @@
         for m, full, prod in zip(mats, rows, prods):
             work[m, top:128, :] = work[m, top:128, :] - prod
 
-    for lo, hi in SEGS:
+    for lo, hi in spans:
         def body(k, _, lo=lo):
             panel(k, lo * 8)
             return 0
         lax.fori_loop(lo, hi, body, 0)
+
 
 def init_work(work, m, gram):
     r = lax.broadcasted_iota(jnp.int32, (128, 128), 0)
@@ -85,39 +86,14 @@
     return lax.dot_general(x, y, (((1,), (1,)), ((), ())), precision=precise, preferred_element_type=jnp.float32)
 
 
-def write_outputs(work, rows, basis_ref, transfer_ref):
-    for c in range(4):
-        basis_ref[c] = times_transposed(rows[c], work[c, :, 128:256])
-    last = lax.axis_index("dev") == lax.axis_size("dev") - 1
-    for n, (left, right, parent) in enumerate(NODES):
-        inverse = work[parent, :, 128:256]
-        for half, child in enumerate((left, right)):
-            made = times_transposed(work[child, :, 0:128], inverse)
-            if n == 3:
-                made = jnp.where(last, 0.0, made)
-            transfer_ref[n, half * 128 : (half + 1) * 128, :] = made
-
-
-def factor_kernel(gram_ref, rows_ref, basis_ref, transfer_ref, work):
-    for m in range(10):
-        init_work(work, m, gram_ref[m])
-    factor_all(work, range(10))
-    write_outputs(work, [rows_ref[c] for c in range(4)], basis_ref, transfer_ref)
-
-
-def factor(grams, rows):
-    vmem = pl.BlockSpec(memory_space=pltpu.VMEM)
-    return pl.pallas_call(
-        factor_kernel,
-        out_shape=(
-            jax.ShapeDtypeStruct((4, 64, 128), jnp.float32),
-            jax.ShapeDtypeStruct((4, 256, 128), jnp.float32),
-        ),
-        in_specs=[vmem, vmem],
-        out_specs=(vmem, vmem),
-        scratch_shapes=[pltpu.VMEM((10, 128, 256), jnp.float32)],
-        name="factor",
-    )(grams, rows)
+def write_node(work, n, transfer_ref):
+    left, right, parent = NODES[n]
+    inverse = work[parent, :, 128:256]
+    for half, child in enumerate((left, right)):
+        made = times_transposed(work[child, :, 0:128], inverse)
+        if n == 3:
+            made = jnp.where(lax.axis_index("dev") == lax.axis_size("dev") - 1, 0.0, made)
+        transfer_ref[n, half * 128 : (half + 1) * 128, :] = made
 
 
 RIGHT, LEFT, DOWN, UP, ACROSS = range(5)
@@ -133,10 +109,36 @@
     return lax.dot_general(x, y, (((1,), (0,)), ((), ())), preferred_element_type=jnp.float32)
 
 
-def gather_kernel(
-    slot_ref, place_ref, rank_ref, omega_ref, u_ref, v_ref, gram_ref, rows_ref,
+def sort_blocks(column_ref, named, places, slots):
+    lane = lax.broadcasted_iota(jnp.int32, (128, 128), 1)
+    down = lax.broadcasted_iota(jnp.int32, (128, 128), 0)
+    named[...] = jnp.full((8, 128), -1, jnp.int32)
+    for i in range(4):
+        named[i : i + 1, 0:80] = column_ref[i]
+    rows = named[...]
+    turned = rows.T
+    places[...] = jnp.full((8, 128), -1, jnp.int32)
+    for i in range(4):
+        row = jnp.broadcast_to(rows[i : i + 1], (128, 128))
+        turn = ((turned[:, i : i + 1] == row) & (down < lane)).astype(jnp.int32)
+        for other in range(i):
+            turn = turn + (turned[:, other : other + 1] == row).astype(jnp.int32)
+        place = jnp.minimum(jnp.sum(turn, axis=0, keepdims=True), 2) * 128 + rows[i : i + 1]
+        places[i : i + 1] = jnp.where(lane[0:1] < 80, place, -1)
+    turned = places[...].T
+    slots[...] = jnp.zeros((8, 128), jnp.int32)
+    for t in range(3):
+        block = jnp.zeros((128, 128), jnp.int32)
+        for i in range(4):
+            block = block + jnp.where(turned[:, i : i + 1] == lane + t * 128, down + i * 80, 0)
+        slots[t : t + 1] = jnp.minimum(jnp.sum(block, axis=0, keepdims=True), 319)
+
+
+def sum_kernel(
+    column_ref, rank_ref, omega_ref, u_ref, v_ref, state_ref, rows_ref, child_ref,
     probe, u_all, v_all, u_high, u_low, coeff, weights,
-    sketch, relay, parts, whole, leaf_gram, leaf_rows, top_gram, tree, eights,
+    sketch, relay, parts, whole, leaf_gram, leaf_rows, top_gram, tree, eights, work, children,
+    named, places, slots, place_at, slot_at,
     load_sem, send_sem, recv_sem, out_sem, in_sem,
 ):
     me = lax.axis_index("dev")
@@ -165,8 +167,15 @@
     peers += [{"grp": (z + n) % 4} for n in range(1, 4)]
     for peer in peers:
         pl.semaphore_signal(barrier, inc=1, device_id=peer, device_id_type=pl.DeviceIdType.MESH)
+    sort_blocks(column_ref, named, places, slots)
+    tables = [
+        pltpu.make_async_copy(places, place_at, load_sem.at[3]),
+        pltpu.make_async_copy(slots, slot_at, load_sem.at[4]),
+    ]
     pl.semaphore_wait(barrier, 13)
     own.wait()
+    for table in tables:
+        table.start()
 
     def move(cluster, way):
         return pltpu.make_async_remote_copy(
@@ -183,19 +192,19 @@
 
     def make_coeff(cluster):
         wide = jnp.concatenate(split_two(probe[cluster]), axis=1)
-        rows = jnp.concatenate([v_all[slot_ref[cluster * 3 + t]] for t in range(3)], axis=0)
+        rows = jnp.concatenate([v_all[slot_at[t, cluster]] for t in range(3)], axis=0)
         high, low = split_two(rows)
         both = bf16_dot(high, wide)
         made = both[:, 0:128] + both[:, 128:256] + bf16_dot(low, wide[:, 0:128])
         packed = jnp.concatenate(split_two(made), axis=1)
         for t in range(3):
-            coeff[cluster * 3 + t] = packed[t * 32 : t * 32 + 32]
+            coeff[t * 128 + cluster] = packed[t * 32 : t * 32 + 32]
 
     rank_row = lax.broadcasted_iota(jnp.int32, (32, 256), 0)
 
     def turn_rows(chunk):
         pieces = [
-            jnp.where(rank_row < rank_ref[chunk * 8 + e], u_all[chunk * 8 + e], 0.0) for e in range(8)
+            jnp.where(rank_row < rank_ref[chunk // 10, chunk % 10 * 8 + e], u_all[chunk * 8 + e], 0.0) for e in range(8)
         ]
         high, low = split_two(jnp.concatenate(pieces, axis=0).T)
         leaf = chunk // 10
@@ -233,6 +242,8 @@
                 work.append(cluster)
         if first and j == 0:
             loads[0].wait()
+            for table in tables:
+                table.wait()
         for cluster in work:
             make_coeff(cluster)
         if chunk is not None:
@@ -275,7 +286,7 @@
 
     def sketch_leaf(leaf):
         for b in range(80):
-            weights[b * 32 : b * 32 + 32, :] = coeff[place_ref[leaf * 80 + b]]
+            weights[b * 32 : b * 32 + 32, :] = coeff[place_at[leaf, b]]
         both = bf16_dot(u_high[leaf], weights[...])
         sketch[leaf] = both[:, 0:128] + both[:, 128:256] + bf16_dot(u_low[leaf], weights[:, 0:128])
 
@@ -340,7 +351,7 @@
         send(whole.at[pl.ds(pl.multiple_of(there * 64, 64), 64)], leaf_rows.at[z], 8 + n, 10 + z, peer)
         for n, there, peer in others
     ]
-    for copy in gram_sends + row_sends:
+    for copy in gram_sends:
         copy.start()
     leaf_rows[z] = whole[pl.ds(pl.multiple_of(z * 64, 64), 64)]
     for _, there, peer in others:
@@ -361,33 +372,19 @@
     )
     for needed, copy in tree_sends:
         pl.when(needed)(copy.start)
-    for c in range(4):
-        gram_ref[c] = leaf_gram[c]
-    gram_ref[4] = first_pair
-    gram_ref[5] = second_pair
-    gram_ref[6] = own_top
+    for copy in row_sends:
+        copy.start()
+    for m, gram in enumerate([leaf_gram[c] for c in range(4)] + [first_pair, second_pair, own_top]):
+        init_work(work, m, gram)
+    factor_all(work, range(7), SEGS[:2])
 
     def arrived(slot):
         send(top_gram, tree.at[slot], 12, 14 + slot, to_after).wait_recv()
         return tree[slot]
 
     def keep(left, right):
-        gram_ref[7] = left
-        gram_ref[8] = right
-        gram_ref[9] = left + right
-
-    @pl.when(e % 2 == 0)
-    def _():
-        keep(own_top, arrived(e + 1))
-
-    @pl.when(e % 4 == 1)
-    def _():
-        keep(arrived(e - 1) + own_top, arrived(e + 1) + arrived(e + 2))
-
-    @pl.when(e == 3)
-    def _():
-        left = arrived(0) + arrived(1) + (arrived(2) + own_top)
-        keep(left, arrived(4) + arrived(5) + (arrived(6) + arrived(7)))
+        children[0] = left
+        children[1] = right
 
     def eight_send(slot, row):
         return send(top_gram, eights.at[y_at], 16 + slot, 22 + y_at, {"dev": row * 8 + 7})
@@ -410,6 +407,34 @@
         for needed, copy in eight_sends:
             pl.when(needed)(copy.start)
 
+    factor_all(work, range(7), SEGS[2:])
+    for _, there, peer in others:
+        send(leaf_rows.at[there], leaf_rows.at[there], 9, 10 + there, peer).wait_recv()
+    results = [
+        pltpu.make_async_copy(work.at[pl.ds(0, 7)], state_ref, load_sem.at[0]),
+        pltpu.make_async_copy(leaf_rows, rows_ref, load_sem.at[1]),
+        pltpu.make_async_copy(children, child_ref, load_sem.at[2]),
+    ]
+    results[0].start()
+    results[1].start()
+
+    @pl.when(e % 2 == 0)
+    def _():
+        keep(own_top, arrived(e + 1))
+
+    @pl.when(e % 4 == 1)
+    def _():
+        keep(arrived(e - 1) + own_top, arrived(e + 1) + arrived(e + 2))
+
+    @pl.when(e == 3)
+    def _():
+        left = arrived(0) + arrived(1) + (arrived(2) + own_top)
+        keep(left, arrived(4) + arrived(5) + (arrived(6) + arrived(7)))
+
+    @pl.when(e == 7)
+    def _():
+        eight = top_gram[...]
+
         def landed(row):
             send(top_gram, eights.at[row], 16, 22 + row, to_after).wait_recv()
             return eights[row]
@@ -438,9 +463,7 @@
         for needed, copy in tree_sends:
             pl.when(needed)(copy.wait_send)
 
-    for _, there, peer in others:
-        send(leaf_rows.at[there], leaf_rows.at[there], 9, 10 + there, peer).wait_recv()
-    rows_ref[...] = leaf_rows[...]
+    results[2].start()
     for copy in [far_out, far_home, near_out, near_home, joint_out, joint_home] + gram_sends + row_sends:
         copy.wait_send()
     for way in range(4):
@@ -454,19 +477,22 @@
         src_ref=probe.at[span], dst_ref=probe.at[span], send_sem=send_sem.at[ACROSS], recv_sem=recv_sem.at[0],
         device_id={"dev": partner}, device_id_type=pl.DeviceIdType.MESH,
     ).wait_send()
-
-
-def sum_sketches(slots, places, ranks, omega, u_rows, v_rows):
+    for result in results:
+        result.wait()
+
+
+def sum_and_factor(columns, ranks, omega, u_rows, v_rows):
     smem = pl.BlockSpec(memory_space=pltpu.SMEM)
     anywhere = pl.BlockSpec(memory_space=pl.ANY)
     return pl.pallas_call(
-        gather_kernel,
+        sum_kernel,
         out_shape=(
-            jax.ShapeDtypeStruct((10, 128, 128), jnp.float32),
+            jax.ShapeDtypeStruct((7, 128, 256), jnp.float32),
             jax.ShapeDtypeStruct((4, 64, 128), jnp.float32),
+            jax.ShapeDtypeStruct((2, 128, 128), jnp.float32),
         ),
-        in_specs=[smem, smem, smem, anywhere, anywhere, anywhere],
-        out_specs=(pl.BlockSpec(memory_space=pltpu.VMEM), pl.BlockSpec(memory_space=pltpu.VMEM)),
+        in_specs=[pl.BlockSpec(memory_space=pltpu.VMEM), smem, anywhere, anywhere, anywhere],
+        out_specs=(anywhere, anywhere, anywhere),
         scratch_shapes=[
             pltpu.VMEM((128, 256, 128), jnp.float32),
             pltpu.VMEM((320, 32, 256), jnp.float32),
@@ -484,7 +510,14 @@
             pltpu.VMEM((128, 128), jnp.float32),
             pltpu.VMEM((8, 128, 128), jnp.float32),
             pltpu.VMEM((4, 128, 128), jnp.float32),
-            pltpu.SemaphoreType.DMA((3,)),
+            pltpu.VMEM((7, 128, 256), jnp.float32),
+            pltpu.VMEM((2, 128, 128), jnp.float32),
+            pltpu.VMEM((8, 128), jnp.int32),
+            pltpu.VMEM((8, 128), jnp.int32),
+            pltpu.VMEM((8, 128), jnp.int32),
+            pltpu.SMEM((8, 128), jnp.int32),
+            pltpu.SMEM((8, 128), jnp.int32),
+            pltpu.SemaphoreType.DMA((5,)),
             pltpu.SemaphoreType.DMA((5,)),
             pltpu.SemaphoreType.DMA((128,)),
             pltpu.SemaphoreType.DMA((18,)),
@@ -493,27 +526,71 @@
         compiler_params=pltpu.CompilerParams(
             collective_id=0, has_side_effects=True, vmem_limit_bytes=62 * 2**20
         ),
-        name="gather",
-    )(slots, places, ranks, omega, u_rows, v_rows)
-
-
-def sort_blocks(columns):
-    named = columns[0, :, :, 0].reshape(320)
-    number = jnp.arange(320, dtype=jnp.int32)
-    same = named[:, None] == named[None, :]
-    turn = jnp.sum((same & (number[None, :] < number[:, None])).astype(jnp.int32), axis=1)
-    places = named * 3 + turn
-    slots = jnp.arange(384, dtype=jnp.int32)
-    hit = places[None, :] == slots[:, None]
-    return jnp.sum(jnp.where(hit, number[None, :], 0), axis=1), places
+        name="recompress",
+    )(columns, ranks, omega, u_rows, v_rows)
+
+
+def finish_kernel(child_ref, state_ref, rows_ref, basis_ref, transfer_ref, work, rows, basis, transfer, sem):
+    loads = [
+        pltpu.make_async_copy(state_ref, work.at[pl.ds(0, 7)], sem.at[0]),
+        pltpu.make_async_copy(rows_ref, rows, sem.at[1]),
+    ]
+    for load in loads:
+        load.start()
+    init_work(work, 7, child_ref[0])
+    init_work(work, 8, child_ref[1])
+    init_work(work, 9, child_ref[0] + child_ref[1])
+    factor_all(work, range(7, 10), SEGS[:1])
+    for load in loads:
+        load.wait()
+    for c in range(4):
+        basis[c] = times_transposed(rows[c], work[c, :, 128:256])
+    for n in range(3):
+        write_node(work, n, transfer)
+    early, late = pl.ds(0, 3), pl.ds(3, 1)
+    stores = [
+        pltpu.make_async_copy(basis, basis_ref, sem.at[2]),
+        pltpu.make_async_copy(transfer.at[early], transfer_ref.at[early], sem.at[3]),
+        pltpu.make_async_copy(transfer.at[late], transfer_ref.at[late], sem.at[4]),
+    ]
+    stores[0].start()
+    stores[1].start()
+    factor_all(work, range(7, 10), SEGS[1:])
+    write_node(work, 3, transfer)
+    stores[2].start()
+    for store in stores:
+        store.wait()
+
+
+def finish(state, rows, children):
+    vmem = pl.BlockSpec(memory_space=pltpu.VMEM)
+    anywhere = pl.BlockSpec(memory_space=pl.ANY)
+    return pl.pallas_call(
+        finish_kernel,
+        out_shape=(
+            jax.ShapeDtypeStruct((4, 64, 128), jnp.float32),
+            jax.ShapeDtypeStruct((4, 256, 128), jnp.float32),
+        ),
+        in_specs=[vmem, anywhere, anywhere],
+        out_specs=(anywhere, anywhere),
+        scratch_shapes=[
+            pltpu.VMEM((10, 128, 256), jnp.float32),
+            pltpu.VMEM((4, 64, 128), jnp.float32),
+            pltpu.VMEM((4, 64, 128), jnp.float32),
+            pltpu.VMEM((4, 256, 128), jnp.float32),
+            pltpu.SemaphoreType.DMA((5,)),
+        ],
+        compiler_params=pltpu.CompilerParams(vmem_limit_bytes=62 * 2**20),
+        name="finish",
+    )(children, state, rows)
 
 
 def on_device(omega, u_factor, v_factor, columns, ranks):
-    slots, places = sort_blocks(columns)
     u_rows = jnp.swapaxes(u_factor, 3, 4).reshape(320, 32, 256)
     v_rows = jnp.swapaxes(v_factor, 3, 4).reshape(320, 32, 256)
-    grams, rows = sum_sketches(slots, places, ranks.reshape(320), omega[0], u_rows, v_rows)
-    return factor(grams, rows)
+    named = jnp.swapaxes(columns[0], 1, 2)
+    state, rows, children = sum_and_factor(named, ranks[0], omega[0], u_rows, v_rows)
+    return finish(state, rows, children)
 
 
 def solution(mesh):

time: 96.6 us -> 91.1 us (0.943)
  the two profiles are of different devices: /device:TPU:15 before, /device:TPU:0 now
where the time goes in v4:
time: 91.1 us; the launch traced here: 90.3 us
  Pallas kernels  89.7 us (98%)
    pallas_call x1, Pallas kernels, sum_and_factor(): pl.pallas_call(sum_kernel, out_shape=(jax.ShapeDtypeStruct((7, 128, 256),...  79.7 us
    pallas_call x1, Pallas kernels, finish(): pl.pallas_call(finish_kernel, out_shape=(jax.ShapeDtypeStruct((4, 64, 128...  10 us

profile of v4, /device:TPU:0, one launch (start us, length us, event | category | flops | bytes accessed | tf_op | source)
XLA Modules:
  0.0 90.3 jit_solution(325089330165194290)
XLA Ops:
  0.6 79.7 %recompress.1 = (f32[7,128,256]{2,1,0:T(8,128)}, f32[4,64,128]{2,1,0:T(8,128)}, f32[2,128,128]{2,1,0:T(8,128)}) custom-call(s32[4,1,80]{2,1,0:T(1,128)} %bitcast.12, s32[4,80]{1,0:T(4,128)} %bitcast.13, f32[4,256,128]{2,1,0:T(8,128)} %bitcast.11, f32[320,32,256]{2,1,0:T(8,128)} %bitcast.9, f32[320,32,256]{2,1,0:T(8,128)} %bitcast.10), custom_call_target="tpu_custom_call" | custom-call | tf_op jit(solution)/shard_map/recompress/pallas_call | solution.py:487
  80.3 10.0 %finish.1 = (f32[4,64,128]{2,1,0:T(8,128)}, f32[4,256,128]{2,1,0:T(8,128)}) custom-call(f32[2,128,128]{2,1,0:T(8,128)} %get-tuple-element.5.child_ref, f32[7,128,256]{2,1,0:T(8,128)} %get-tuple-element.6.state_ref, f32[4,64,128]{2,1,0:T(8,128)} %get-tuple-element.7.rows_ref), custom_call_target="tpu_custom_call" | custom-call | tf_op jit(solution)/shard_map/finish/pallas_call | solution.py:568

commit v5 on v4

--- a/solution.py
+++ b/solution.py
@@ -9,14 +9,15 @@
 precise = lax.Precision.HIGHEST
 
 
-GROUP = 5
-SEGS = ((0, 4), (4, 8), (8, 12), (12, 16))
+SEGS = ((0, 2), (2, 4), (4, 6), (6, 8))
+
 
 def pick_lane(x, lane):
     idx = jnp.full(x.shape, lane, jnp.int32)
     return jnp.take_along_axis(x, idx, axis=1)
 
-def factor_all(work, mats, spans=SEGS):
+
+def make_panel(work, mats, group):
     sub = lax.broadcasted_iota(jnp.int32, (8, 128), 0)
     lane = lax.broadcasted_iota(jnp.int32, (8, 128), 1)
 
@@ -27,47 +28,71 @@
         return h, d, rest - d
 
     def panel(k, top):
-        base = pl.multiple_of(k * 8, 8)
-        raw = [work[m, pl.ds(base, 8), :] for m in mats]
-        keep = lane >= base + sub
-        below = lane >= base + 8
+        base = k * 16 if isinstance(k, int) else pl.multiple_of(k * 16, 16)
+        raw = [work[m, pl.ds(base, 16), :] for m in mats]
         prods = []
         rows = []
-        for g in range(0, len(mats), GROUP):
-            part = raw[g:g + GROUP]
-            ps = [x[:, 0:128] for x in part]
-            qs = [x[:, 128:256] for x in part]
-            cols = [[pick_lane(p, base + r) for r in range(8)] for p in ps]
-            for r in range(8):
-                for i in range(len(part)):
-                    c = cols[i][r]
-                    inv = lax.rsqrt(jnp.broadcast_to(c[r:r + 1], (8, 128)))
-                    cs = c * inv
-                    prow = ps[i][r:r + 1] * inv
-                    qrow = qs[i][r:r + 1] * inv
-                    cz = jnp.where(sub > r, cs, 0.0)
-                    ps[i] = jnp.where(sub == r, prow, ps[i] - cz * prow)
-                    qs[i] = jnp.where(sub == r, qrow, qs[i] - cz * qrow)
-                    for t in range(r + 1, 8):
-                        cols[i][t] = cols[i][t] - cs * cs[t:t + 1]
-            for i in range(len(part)):
-                p = jnp.where(keep, ps[i], 0.0)
-                full = jnp.concatenate([p, qs[i]], axis=1)
+        for g in range(0, len(mats), group):
+            part = raw[g : g + group]
+            ps = [[x[0:8, 0:128], x[8:16, 0:128]] for x in part]
+            qs = [[x[0:8, 128:256], x[8:16, 128:256]] for x in part]
+            high = [[pick_lane(p[0], base + r) for r in range(8)] for p in ps]
+            low = [[pick_lane(p[1], base + r) for r in range(16)] for p in ps]
+            for r in range(16):
+                h, n = r // 8, r % 8
+                for p, q, up, down in zip(ps, qs, high, low):
+                    pivot = (up if h == 0 else down)[r][n : n + 1]
+                    inv = lax.rsqrt(jnp.broadcast_to(pivot, (8, 128)))
+                    prow = p[h][n : n + 1] * inv
+                    qrow = q[h][n : n + 1] * inv
+                    below = down[r] * inv
+                    if h == 0:
+                        here = up[r] * inv
+                        p[1] = p[1] - below * prow
+                        q[1] = q[1] - below * qrow
+                        for t in range(r + 1, 8):
+                            up[t] = up[t] - here * here[t : t + 1]
+                            down[t] = down[t] - below * here[t : t + 1]
+                    else:
+                        here = below
+                    for t in range(max(r + 1, 8), 16):
+                        down[t] = down[t] - below * below[t - 8 : t - 7]
+                    rest = jnp.where(sub > n, here, 0.0)
+                    p[h] = jnp.where(sub == n, prow, p[h] - rest * prow)
+                    q[h] = jnp.where(sub == n, qrow, q[h] - rest * qrow)
+            for p, q in zip(ps, qs):
+                both = [jnp.where(lane >= base + 8 * h + sub, p[h], 0.0) for h in range(2)]
+                full = jnp.concatenate([jnp.concatenate(both, axis=0), jnp.concatenate(q, axis=0)], axis=1)
                 rows.append(full)
-                ph, pd, pe = split(jnp.where(below, p, 0.0))
+                if top == 128:
+                    continue
+                after = [jnp.where(lane >= base + 16, x, 0.0) for x in both]
+                ph, pd, pe = split(jnp.concatenate(after, axis=0))
                 fh, fd, fe = split(full)
                 left = jnp.concatenate([ph, ph, pd, ph, pe, pd], axis=0)
                 right = jnp.concatenate([fh, fd, fh, fe, fh, fd], axis=0)
-                leftT = left.T[top:].astype(jnp.bfloat16)
-                prods.append(lax.dot_general(leftT, right.astype(jnp.bfloat16), (((1,), (0,)), ((), ())), preferred_element_type=jnp.float32))
-        for m, full, prod in zip(mats, rows, prods):
-            work[m, pl.ds(base, 8), :] = full
-        for m, full, prod in zip(mats, rows, prods):
+                turned = left.T[top:].astype(jnp.bfloat16)
+                prods.append(
+                    lax.dot_general(
+                        turned,
+                        right.astype(jnp.bfloat16),
+                        (((1,), (0,)), ((), ())),
+                        preferred_element_type=jnp.float32,
+                    )
+                )
+        for m, full in zip(mats, rows):
+            work[m, pl.ds(base, 16), :] = full
+        for m, prod in zip(mats, prods):
             work[m, top:128, :] = work[m, top:128, :] - prod
 
+    return panel
+
+
+def factor_span(work, mats, spans):
+    panel = make_panel(work, mats, 4)
     for lo, hi in spans:
         def body(k, _, lo=lo):
-            panel(k, lo * 8)
+            panel(k, lo * 16)
             return 0
         lax.fori_loop(lo, hi, body, 0)
 
@@ -376,7 +401,7 @@
         copy.start()
     for m, gram in enumerate([leaf_gram[c] for c in range(4)] + [first_pair, second_pair, own_top]):
         init_work(work, m, gram)
-    factor_all(work, range(7), SEGS[:2])
+    factor_span(work, range(7), SEGS[:2])
 
     def arrived(slot):
         send(top_gram, tree.at[slot], 12, 14 + slot, to_after).wait_recv()
@@ -407,7 +432,7 @@
         for needed, copy in eight_sends:
             pl.when(needed)(copy.start)
 
-    factor_all(work, range(7), SEGS[2:])
+    factor_span(work, range(7), SEGS[2:])
     for _, there, peer in others:
         send(leaf_rows.at[there], leaf_rows.at[there], 9, 10 + there, peer).wait_recv()
     results = [
@@ -540,13 +565,20 @@
     init_work(work, 7, child_ref[0])
     init_work(work, 8, child_ref[1])
     init_work(work, 9, child_ref[0] + child_ref[1])
-    factor_all(work, range(7, 10), SEGS[:1])
+    panel = make_panel(work, range(7, 10), 3)
+    panel(0, 16)
+    panel(1, 32)
     for load in loads:
         load.wait()
+    panel(2, 48)
     for c in range(4):
         basis[c] = times_transposed(rows[c], work[c, :, 128:256])
-    for n in range(3):
-        write_node(work, n, transfer)
+    panel(3, 64)
+    write_node(work, 0, transfer)
+    panel(4, 80)
+    write_node(work, 1, transfer)
+    panel(5, 96)
+    write_node(work, 2, transfer)
     early, late = pl.ds(0, 3), pl.ds(3, 1)
     stores = [
         pltpu.make_async_copy(basis, basis_ref, sem.at[2]),
@@ -555,7 +587,8 @@
     ]
     stores[0].start()
     stores[1].start()
-    factor_all(work, range(7, 10), SEGS[1:])
+    panel(6, 112)
+    panel(7, 128)
     write_node(work, 3, transfer)
     stores[2].start()
     for store in stores:

time: 91.1 us -> 87.4 us (0.959)
  Pallas kernels: 89.7 us -> 85.8 us
    pallas_call x1, Pallas kernels: 10 us -> 6.63 us  [finish(): pl.pallas_call(finish_kernel, out_shape=(jax.ShapeDtypeStruct((4, 64, 128...]
where the time goes in v5:
time: 87.4 us; the launch traced here: 86.6 us
  Pallas kernels  85.8 us (98%)
    pallas_call x1, Pallas kernels, sum_and_factor(): pl.pallas_call(sum_kernel, out_shape=(jax.ShapeDtypeStruct((7, 128, 256),...  79.2 us
    pallas_call x1, Pallas kernels, finish(): pl.pallas_call(finish_kernel, out_shape=(jax.ShapeDtypeStruct((4, 64, 128...  6.63 us

profile of v5, /device:TPU:0, one launch (start us, length us, event | category | flops | bytes accessed | tf_op | source)
XLA Modules:
  0.0 86.6 jit_solution(22246345341140780)
XLA Ops:
  0.6 79.2 %recompress.1 = (f32[7,128,256]{2,1,0:T(8,128)}, f32[4,64,128]{2,1,0:T(8,128)}, f32[2,128,128]{2,1,0:T(8,128)}) custom-call(s32[4,1,80]{2,1,0:T(1,128)} %bitcast.12, s32[4,80]{1,0:T(4,128)} %bitcast.13, f32[4,256,128]{2,1,0:T(8,128)} %bitcast.11, f32[320,32,256]{2,1,0:T(8,128)} %bitcast.9, f32[320,32,256]{2,1,0:T(8,128)} %bitcast.10), custom_call_target="tpu_custom_call" | custom-call | tf_op jit(solution)/shard_map/recompress/pallas_call | solution.py:512
  79.9 6.6 %finish.1 = (f32[4,64,128]{2,1,0:T(8,128)}, f32[4,256,128]{2,1,0:T(8,128)}) custom-call(f32[2,128,128]{2,1,0:T(8,128)} %get-tuple-element.5.child_ref, f32[7,128,256]{2,1,0:T(8,128)} %get-tuple-element.6.state_ref, f32[4,64,128]{2,1,0:T(8,128)} %get-tuple-element.7.rows_ref), custom_call_target="tpu_custom_call" | custom-call | tf_op jit(solution)/shard_map/finish/pallas_call | solution.py:601

commit v6 on v5

--- a/solution.py
+++ b/solution.py
@@ -7,9 +7,6 @@
 from jax.sharding import PartitionSpec as P
 
 precise = lax.Precision.HIGHEST
-
-
-SEGS = ((0, 2), (2, 4), (4, 6), (6, 8))
 
 
 def pick_lane(x, lane):
@@ -88,15 +85,6 @@
     return panel
 
 
-def factor_span(work, mats, spans):
-    panel = make_panel(work, mats, 4)
-    for lo, hi in spans:
-        def body(k, _, lo=lo):
-            panel(k, lo * 16)
-            return 0
-        lax.fori_loop(lo, hi, body, 0)
-
-
 def init_work(work, m, gram):
     r = lax.broadcasted_iota(jnp.int32, (128, 128), 0)
     c = lax.broadcasted_iota(jnp.int32, (128, 128), 1)
@@ -328,20 +316,25 @@
     top, bottom = pl.ds(0, 128), pl.ds(128, 128)
     after, across_z, before = [(z + n) % 4 for n in (1, 2, 3)]
     to_after, to_across, to_before = [{"grp": n} for n in (after, across_z, before)]
-    far_out = send(sketch.at[across_z, top], relay.at[0], 0, 0, to_after)
-    far_home = send(sketch.at[across_z, bottom], relay.at[1], 1, 1, to_before)
+    halves = [(pl.ds(64 * h, 64), pl.ds(128 + 64 * h, 64), h) for h in range(2)]
+    far_out = [send(sketch.at[across_z, a], relay.at[0, a], 18 * h, 26 * h, to_after) for a, _, h in halves]
+    far_home = [
+        send(sketch.at[across_z, b], relay.at[1, a], 1 + 18 * h, 1 + 26 * h, to_before) for a, b, h in halves
+    ]
     near_out = send(sketch.at[after, bottom], parts.at[0], 2, 2, to_after)
     near_home = send(sketch.at[before, top], parts.at[1], 3, 3, to_before)
-    joint_out = send(sketch.at[after, top], parts.at[2], 4, 4, to_after)
-    joint_home = send(sketch.at[before, bottom], parts.at[3], 5, 5, to_before)
+    joint_out = [send(sketch.at[after, a], parts.at[2, a], 4 + 16 * h, 4 + 24 * h, to_after) for a, _, h in halves]
+    joint_home = [
+        send(sketch.at[before, b], parts.at[3, a], 5 + 16 * h, 5 + 24 * h, to_before) for a, b, h in halves
+    ]
 
     def leaf_step(n, carry):
         sketch_leaf((z + jnp.where(n == 0, 2, jnp.where(n == 1, 1, jnp.where(n == 2, 3, 0)))) % 4)
 
         @pl.when(n == 0)
         def _():
-            far_out.start()
-            far_home.start()
+            for copy in (far_out[0], far_home[0], far_out[1], far_home[1]):
+                copy.start()
 
         @pl.when(n == 1)
         def _():
@@ -354,17 +347,21 @@
         return carry
 
     lax.fori_loop(0, 4, leaf_step, 0)
-    far_out.wait_recv()
-    sketch[after, 0:128] = sketch[after, 0:128] + relay[0]
-    joint_out.start()
-    far_home.wait_recv()
-    sketch[before, 128:256] = sketch[before, 128:256] + relay[1]
-    joint_home.start()
+    for h in range(2):
+        lo, hi = 64 * h, 64 * h + 64
+        far_out[h].wait_recv()
+        sketch[after, lo:hi] = sketch[after, lo:hi] + relay[0, lo:hi]
+        joint_out[h].start()
+        far_home[h].wait_recv()
+        sketch[before, 128 + lo : 128 + hi] = sketch[before, 128 + lo : 128 + hi] + relay[1, lo:hi]
+        joint_home[h].start()
     near_out.wait_recv()
     near_home.wait_recv()
-    joint_out.wait_recv()
+    for copy in joint_out:
+        copy.wait_recv()
     whole[0:128] = sketch[z, 0:128] + parts[1] + parts[2]
-    joint_home.wait_recv()
+    for copy in joint_home:
+        copy.wait_recv()
     whole[128:256] = sketch[z, 128:256] + parts[0] + parts[3]
     flat = whole[...]
     leaf_gram[z] = lax.dot_general(
@@ -401,7 +398,9 @@
         copy.start()
     for m, gram in enumerate([leaf_gram[c] for c in range(4)] + [first_pair, second_pair, own_top]):
         init_work(work, m, gram)
-    factor_span(work, range(7), SEGS[:2])
+    panel = make_panel(work, range(7), 7)
+    for k in range(4):
+        panel(k, k * 16 + 16)
 
     def arrived(slot):
         send(top_gram, tree.at[slot], 12, 14 + slot, to_after).wait_recv()
@@ -432,7 +431,8 @@
         for needed, copy in eight_sends:
             pl.when(needed)(copy.start)
 
-    factor_span(work, range(7), SEGS[2:])
+    for k in range(4, 8):
+        panel(k, k * 16 + 16)
     for _, there, peer in others:
         send(leaf_rows.at[there], leaf_rows.at[there], 9, 10 + there, peer).wait_recv()
     results = [
@@ -489,7 +489,7 @@
             pl.when(needed)(copy.wait_send)
 
     results[2].start()
-    for copy in [far_out, far_home, near_out, near_home, joint_out, joint_home] + gram_sends + row_sends:
+    for copy in far_out + far_home + [near_out, near_home] + joint_out + joint_home + gram_sends + row_sends:
         copy.wait_send()
     for way in range(4):
         span = pl.ds(0, 15)
@@ -545,8 +545,8 @@
             pltpu.SemaphoreType.DMA((5,)),
             pltpu.SemaphoreType.DMA((5,)),
             pltpu.SemaphoreType.DMA((128,)),
-            pltpu.SemaphoreType.DMA((18,)),
-            pltpu.SemaphoreType.DMA((26,)),
+            pltpu.SemaphoreType.DMA((22,)),
+            pltpu.SemaphoreType.DMA((30,)),
         ],
         compiler_params=pltpu.CompilerParams(
             collective_id=0, has_side_effects=True, vmem_limit_bytes=62 * 2**20

time: 87.4 us -> 86.4 us (0.989)
  Pallas kernels: 85.8 us -> 84.8 us
    pallas_call x1, Pallas kernels: 79.2 us -> 78.1 us  [sum_and_factor(): pl.pallas_call(sum_kernel, out_shape=(jax.ShapeDtypeStruct((7, 128, 256),...]
where the time goes in v6:
time: 86.4 us; the launch traced here: 85.6 us
  Pallas kernels  84.8 us (98%)
    pallas_call x1, Pallas kernels, sum_and_factor(): pl.pallas_call(sum_kernel, out_shape=(jax.ShapeDtypeStruct((7, 128, 256),...  78.1 us
    pallas_call x1, Pallas kernels, finish(): pl.pallas_call(finish_kernel, out_shape=(jax.ShapeDtypeStruct((4, 64, 128...  6.63 us

profile of v6, /device:TPU:0, one launch (start us, length us, event | category | flops | bytes accessed | tf_op | source)
XLA Modules:
  0.0 85.6 jit_solution(13590777932486507999)
XLA Ops:
  0.6 78.1 %recompress.1 = (f32[7,128,256]{2,1,0:T(8,128)}, f32[4,64,128]{2,1,0:T(8,128)}, f32[2,128,128]{2,1,0:T(8,128)}) custom-call(s32[4,1,80]{2,1,0:T(1,128)} %bitcast.12, s32[4,80]{1,0:T(4,128)} %bitcast.13, f32[4,256,128]{2,1,0:T(8,128)} %bitcast.11, f32[320,32,256]{2,1,0:T(8,128)} %bitcast.9, f32[320,32,256]{2,1,0:T(8,128)} %bitcast.10), custom_call_target="tpu_custom_call" | custom-call | tf_op jit(solution)/shard_map/recompress/pallas_call | solution.py:512
  78.8 6.6 %finish.1 = (f32[4,64,128]{2,1,0:T(8,128)}, f32[4,256,128]{2,1,0:T(8,128)}) custom-call(f32[2,128,128]{2,1,0:T(8,128)} %get-tuple-element.5.child_ref, f32[7,128,256]{2,1,0:T(8,128)} %get-tuple-element.6.state_ref, f32[4,64,128]{2,1,0:T(8,128)} %get-tuple-element.7.rows_ref), custom_call_target="tpu_custom_call" | custom-call | tf_op jit(solution)/shard_map/finish/pallas_call | solution.py:601
